TPU v7x, 32 devices: a whole 2x2x4 slice. The times are simulated.
32 devices in a mesh: dp: 2 (over x), ctx: 2 (over y), expert: 8 (over z, core).
Axes of the slice: x: 2, y: 2, z: 4, core: 2. Of those that a mesh axis runs over, the one named last changes fastest.
Arguments:
- layer_input: bfloat16 [16, 256, 2048], P(('dp', 'expert'), 'ctx'), may hold values from -6 to 6
- cotangent: bfloat16 [16, 256, 2048], P(('dp', 'expert'), 'ctx'), may hold values from -6 to 6
- routes: int32 [16, 256, 6], P(('dp', 'expert'), 'ctx'), may hold values from 0 to 15, all different within a row; in each aligned block of 128 rows (0 to 127, 128 to 255, ..., all dimensions but the last counted through in order) at most 64 rows name the same one
- attn_gain: float32 [2048], replicated, may hold values from 0.5 to 1.5
- w_query: bfloat16 [2048, 3072], P('expert'), may hold values from -0.125 to 0.125
- w_latent: bfloat16 [2048, 576], P('expert'), may hold values from -0.125 to 0.125
- latent_gain: float32 [512], replicated, may hold values from 0.5 to 1.5
- w_expand: bfloat16 [512, 4096], P('expert'), may hold values from -0.25 to 0.25
- w_output: bfloat16 [2048, 2048], P('expert'), may hold values from -0.5 to 0.5
- ffn_gain: float32 [2048], replicated, may hold values from 0.5 to 1.5
- w_router: bfloat16 [2048, 16], P('expert'), may hold values from -0.125 to 0.125
- w_shared_in: bfloat16 [2048, 5632], P('expert'), may hold values from -0.125 to 0.125
- w_shared_out: bfloat16 [2816, 2048], P('expert'), may hold values from -0.109375 to 0.109375
- w_expert_in: bfloat16 [16, 2, 1408, 2048], P('expert', None, ('dp', 'ctx')), may hold values from -0.125 to 0.125
- w_expert_out: bfloat16 [16, 1408, 2048], P('expert', ('dp', 'ctx')), may hold values from -2.5 to 2.5
Outputs:
- layer_output: bfloat16 [16, 256, 2048], P(('dp', 'expert'), 'ctx')
- grad_input: bfloat16 [16, 256, 2048], P(('dp', 'expert'), 'ctx')
- grad_attn_gain: float32 [2048], P('expert')
- grad_w_query: float32 [2048, 3072], P('expert')
- grad_w_latent: float32 [2048, 576], P('expert')
- grad_latent_gain: float32 [512], P('expert')
- grad_w_expand: float32 [512, 4096], P('expert')
- grad_w_output: float32 [2048, 2048], P('expert')
- grad_ffn_gain: float32 [2048], P('expert')
- grad_w_router: float32 [2048, 16], P('expert')
- grad_w_shared_in: float32 [2048, 5632], P('expert')
- grad_w_shared_out: float32 [2816, 2048], P('expert')
- grad_w_expert_in: float32 [16, 2, 1408, 2048], P('expert', None, ('dp', 'ctx'))
- grad_w_expert_out: float32 [16, 1408, 2048], P('expert', ('dp', 'ctx'))
Inputs may be any that keep to these rules, and one draw needn't show every extreme that they name: `routes`: each token names 6 different experts; among the 128 tokens of one device no expert is named more than 64 times, a bound that some block reaches.
All inputs are finite; a program needn't handle non-finite values.
Results may differ from a plain program's by a relative error of at most 0.028.
Values may be sent and summed in bfloat16 or wider, within the bound.
A program may use at most 384 MiB of HBM per device.

v0:
```python
import math

import jax
import jax.numpy as jnp
from jax import lax
from jax.sharding import PartitionSpec as P

HEADS = 16
NOPE = 128
ROPE = 64
VH = 128
KV = 512
TOP = 6


EPS = 1e-06


def normalize(operand):
    factor = lax.rsqrt(jnp.mean(operand * operand, axis=-1, keepdims=True) + EPS)
    return (operand * factor, factor)


def norm_back(grad_out, normed, factor, gain_row):
    inner_sums = grad_out * gain_row
    grad_in = factor * (inner_sums - normed * jnp.mean(inner_sums * normed, axis=-1, keepdims=True))
    return (grad_in, jnp.sum(grad_out * normed, axis=0))


def rotate(operand, cosine, sine_part):
    half_width = operand.shape[-1] // 2
    former = operand[..., :half_width]
    latter = operand[..., half_width:]
    return jnp.concatenate(
        [former * cosine - latter * sine_part, latter * cosine + former * sine_part], axis=-1
    )


def across(left_side, right_side):
    return lax.dot_general(
        left_side, right_side, (((0,), (0,)), ((), ())), preferred_element_type=jnp.float32
    )


def against(left_side, right_side):
    return lax.dot_general(
        left_side, right_side, (((1,), (1,)), ((), ())), preferred_element_type=jnp.float32
    )


def silu_parts(operand):
    sigmoid_of = jax.nn.sigmoid(operand)
    return (operand * sigmoid_of, sigmoid_of * (1.0 + operand * (1.0 - sigmoid_of)))


def to_experts(buffer):
    return lax.all_to_all(buffer, "expert", split_axis=0, concat_axis=2, tiled=True)


def from_experts(buffer):
    return lax.all_to_all(buffer, "expert", split_axis=2, concat_axis=0, tiled=True)


def share_rows(row_block):
    return lax.all_gather(row_block, ("dp", "ctx"), axis=1, tiled=True)


def sum_rows(partial_value):
    return lax.psum_scatter(
        partial_value.astype(jnp.bfloat16), ("dp", "ctx"), scatter_dimension=1, tiled=True
    ).astype(jnp.float32)


def key_scores(query_r, keys_nope, keys_rope, allowed, scale_factor):
    scores = jnp.einsum(
        "qhd,khd->hqk", query_r[..., :NOPE], keys_nope, preferred_element_type=jnp.float32
    )
    scores = scores + jnp.einsum(
        "qhd,kd->hqk", query_r[..., NOPE:], keys_rope, preferred_element_type=jnp.float32
    )
    return jnp.where(allowed[None], scores * scale_factor, -1e30)


def body(
    layer_input,
    cotangent,
    routes,
    attn_gain,
    w_query,
    w_latent,
    latent_gain,
    w_expand,
    w_output,
    ffn_gain,
    w_router,
    w_shared_in,
    w_shared_out,
    w_expert_in,
    w_expert_out,
):
    (
        weight_query,
        weight_latent,
        weight_expand,
        weight_output,
        weight_router,
        weight_shared_in,
        weight_shared_out,
    ) = (
        lax.all_gather(w_query, "expert", axis=0, tiled=True),
        lax.all_gather(w_latent, "expert", axis=0, tiled=True),
        lax.all_gather(w_expand, "expert", axis=0, tiled=True),
        lax.all_gather(w_output, "expert", axis=0, tiled=True),
        lax.all_gather(w_router, "expert", axis=0, tiled=True),
        lax.all_gather(w_shared_in, "expert", axis=0, tiled=True),
        lax.all_gather(w_shared_out, "expert", axis=0, tiled=True),
    )
    tokens = layer_input[0].astype(jnp.float32)
    tok_count = tokens.shape[0]
    row_width = tokens.shape[1]
    experts = weight_router.shape[1]
    groups = lax.axis_size("expert")
    local_experts = experts // groups
    capacity = tok_count * TOP * 4 // (3 * experts)
    assigns = tok_count * TOP
    shared_width = weight_shared_out.shape[0]
    places = lax.axis_index("ctx") * tok_count + jnp.arange(tok_count, dtype=jnp.int32)
    inverse = 10000.0 ** (-jnp.arange(0, ROPE, 2).astype(jnp.float32) / ROPE)
    angles = places.astype(jnp.float32)[:, None] * inverse[None, :]
    cosine = jnp.cos(angles)
    sine_part = jnp.sin(angles)
    normed_one, factor_one = normalize(tokens)
    hidden_one = (normed_one * attn_gain).astype(jnp.bfloat16)
    queries = jnp.dot(hidden_one, weight_query, preferred_element_type=jnp.float32).reshape(
        tok_count, HEADS, NOPE + ROPE
    )
    query_r = jnp.concatenate(
        [
            queries[..., :NOPE],
            rotate(queries[..., NOPE:], cosine[:, None, :], sine_part[:, None, :]),
        ],
        axis=-1,
    ).astype(jnp.bfloat16)
    latent = jnp.dot(hidden_one, weight_latent, preferred_element_type=jnp.float32)
    normed_lat, factor_lat = normalize(latent[:, :KV])
    compressed = (normed_lat * latent_gain).astype(jnp.bfloat16)
    key_rope = rotate(latent[:, KV:], cosine, sine_part).astype(jnp.bfloat16)
    packed = jnp.concatenate([compressed, key_rope], axis=1)
    all_keys = lax.all_gather(packed, "ctx", axis=0, tiled=True)
    every_comp = all_keys[:, :KV]
    every_rope = all_keys[:, KV:]
    expanded = (
        jnp.dot(every_comp, weight_expand, preferred_element_type=jnp.float32)
        .astype(jnp.bfloat16)
        .reshape(-1, HEADS, NOPE + VH)
    )
    keys_nope = expanded[..., :NOPE]
    values = expanded[..., NOPE:]
    scale_factor = 1.0 / math.sqrt(NOPE + ROPE)
    allowed = jnp.arange(all_keys.shape[0], dtype=jnp.int32)[None, :] <= places[:, None]
    scores = key_scores(query_r, keys_nope, every_rope, allowed, scale_factor)
    highest = jnp.max(scores, axis=-1, keepdims=True)
    exponent = jnp.exp(scores - highest)
    totals = jnp.sum(exponent, axis=-1, keepdims=True)
    logsum = highest + jnp.log(totals)
    weights = (exponent / totals).astype(jnp.bfloat16)
    mixed_heads = (
        jnp.einsum("hqk,khd->qhd", weights, values, preferred_element_type=jnp.float32)
        .reshape(tok_count, HEADS * VH)
        .astype(jnp.bfloat16)
    )
    first_sum = tokens + jnp.dot(mixed_heads, weight_output, preferred_element_type=jnp.float32)
    normed_two, factor_two = normalize(first_sum)
    hidden_two = (normed_two * ffn_gain).astype(jnp.bfloat16)
    logits = jnp.dot(hidden_two, weight_router, preferred_element_type=jnp.float32)
    router_top = jnp.max(logits, axis=-1, keepdims=True)
    router_exp = jnp.exp(logits - router_top)
    router = router_exp / jnp.sum(router_exp, axis=-1, keepdims=True)
    own_routes = routes[0]
    chosen = own_routes[:, :, None] == jnp.arange(experts, dtype=jnp.int32)[None, None, :]
    picked = jnp.sum(jnp.where(chosen, router[:, None, :], 0.0), axis=2)
    shared_gu = jnp.dot(hidden_two, weight_shared_in, preferred_element_type=jnp.float32)
    shared_gate = shared_gu[:, :shared_width]
    shared_up = shared_gu[:, shared_width:]
    shared_silu, shared_slope = silu_parts(shared_gate)
    shared_act = (shared_silu * shared_up).astype(jnp.bfloat16)
    shared = jnp.dot(shared_act, weight_shared_out, preferred_element_type=jnp.float32)
    picked_ids = own_routes.reshape(-1)
    onehot = (picked_ids[:, None] == jnp.arange(experts, dtype=jnp.int32)[None, :]).astype(
        jnp.int32
    )
    position = jnp.sum((jnp.cumsum(onehot, axis=0) - onehot) * onehot, axis=1)
    target = picked_ids * capacity + position
    holder = (
        jnp.full((experts * capacity,), assigns, jnp.int32)
        .at[target]
        .set(jnp.arange(assigns, dtype=jnp.int32))
    )
    padded = jnp.concatenate([hidden_two, jnp.zeros((1, row_width), jnp.bfloat16)], axis=0)
    outgoing = padded[holder // TOP].reshape(groups, local_experts, capacity, row_width)
    incoming = to_experts(outgoing)[0]
    expert_input = share_rows(incoming)
    paired = jnp.einsum(
        "erd,egfd->ergf", expert_input, w_expert_in, preferred_element_type=jnp.float32
    )
    expert_gate = paired[:, :, 0]
    expert_up = paired[:, :, 1]
    expert_silu, expert_slope = silu_parts(expert_gate)
    expert_act = (expert_silu * expert_up).astype(jnp.bfloat16)
    partial_value = jnp.einsum(
        "erf,efd->erd", expert_act, w_expert_out, preferred_element_type=jnp.float32
    )
    expert_out = sum_rows(partial_value).astype(jnp.bfloat16)
    returned = from_experts(expert_out[None]).reshape(experts * capacity, row_width)
    gathered = returned[target].reshape(tok_count, TOP, row_width).astype(jnp.float32)
    routed = jnp.sum(picked[:, :, None] * gathered, axis=1)
    output = (first_sum + shared + routed).astype(jnp.bfloat16)[None]
    grad_out = cotangent[0].astype(jnp.float32)
    grad_picked = jnp.sum(grad_out[:, None, :] * gathered, axis=2)
    sending = (
        (picked[:, :, None] * grad_out[:, None, :]).astype(jnp.bfloat16).reshape(assigns, row_width)
    )
    sending = jnp.concatenate([sending, jnp.zeros((1, row_width), jnp.bfloat16)], axis=0)[holder]
    grad_expert_out = to_experts(sending.reshape(groups, local_experts, capacity, row_width))[0]
    grad_expert_out = share_rows(grad_expert_out)
    grad_act = jnp.einsum(
        "erd,efd->erf", grad_expert_out, w_expert_out, preferred_element_type=jnp.float32
    )
    grad_weight_out = jnp.einsum(
        "erf,erd->efd", expert_act, grad_expert_out, preferred_element_type=jnp.float32
    )
    grad_paired = jnp.stack(
        [grad_act * expert_up * expert_slope, grad_act * expert_silu], axis=2
    ).astype(jnp.bfloat16)
    grad_weight_in = jnp.einsum(
        "ergf,erd->egfd", grad_paired, expert_input, preferred_element_type=jnp.float32
    )
    grad_input_part = jnp.einsum(
        "ergf,egfd->erd", grad_paired, w_expert_in, preferred_element_type=jnp.float32
    )
    grad_rows_sum = sum_rows(grad_input_part)
    grad_back = from_experts(grad_rows_sum.astype(jnp.bfloat16)[None]).reshape(
        experts * capacity, row_width
    )
    grad_hidden_two = jnp.sum(
        grad_back[target].reshape(tok_count, TOP, row_width).astype(jnp.float32), axis=1
    )
    grad_router = jnp.sum(jnp.where(chosen, grad_picked[:, :, None], 0.0), axis=1)
    grad_logits = (
        router * (grad_router - jnp.sum(router * grad_router, axis=1, keepdims=True))
    ).astype(jnp.bfloat16)
    grad_router_weight = across(hidden_two, grad_logits)
    grad_hidden_two = grad_hidden_two + against(grad_logits, weight_router)
    grad_low = grad_out.astype(jnp.bfloat16)
    grad_shared_out = across(shared_act, grad_low)
    grad_shared_act = against(grad_low, weight_shared_out)
    grad_shared_gu = jnp.concatenate(
        [grad_shared_act * shared_up * shared_slope, grad_shared_act * shared_silu], axis=1
    ).astype(jnp.bfloat16)
    grad_shared_in = across(hidden_two, grad_shared_gu)
    grad_hidden_two = grad_hidden_two + against(grad_shared_gu, weight_shared_in)
    grad_first_norm, grad_ffn = norm_back(grad_hidden_two, normed_two, factor_two, ffn_gain)
    grad_first = grad_out + grad_first_norm
    grad_first_low = grad_first.astype(jnp.bfloat16)
    grad_output_weight = across(mixed_heads, grad_first_low)
    grad_mixed = (
        against(grad_first_low, weight_output).astype(jnp.bfloat16).reshape(tok_count, HEADS, VH)
    )
    prob_rows = jnp.exp(key_scores(query_r, keys_nope, every_rope, allowed, scale_factor) - logsum)
    grad_weights = jnp.einsum(
        "qhd,khd->hqk", grad_mixed, values, preferred_element_type=jnp.float32
    )
    grad_scores = (
        prob_rows * (grad_weights - jnp.sum(prob_rows * grad_weights, axis=-1, keepdims=True))
    ).astype(jnp.bfloat16)
    grad_query_nope = (
        jnp.einsum("hqk,khd->qhd", grad_scores, keys_nope, preferred_element_type=jnp.float32)
        * scale_factor
    )
    grad_query_rope = (
        jnp.einsum("hqk,kd->qhd", grad_scores, every_rope, preferred_element_type=jnp.float32)
        * scale_factor
    )
    grad_keys_nope = (
        jnp.einsum(
            "hqk,qhd->khd", grad_scores, query_r[..., :NOPE], preferred_element_type=jnp.float32
        )
        * scale_factor
    )
    grad_keys_rope = (
        jnp.einsum(
            "hqk,qhd->kd", grad_scores, query_r[..., NOPE:], preferred_element_type=jnp.float32
        )
        * scale_factor
    )
    grad_values = jnp.einsum(
        "hqk,qhd->khd", weights, grad_mixed, preferred_element_type=jnp.float32
    )
    grad_expanded = (
        jnp.concatenate([grad_keys_nope, grad_values], axis=-1)
        .reshape(all_keys.shape[0], -1)
        .astype(jnp.bfloat16)
    )
    grad_expand_weight = across(every_comp, grad_expanded)
    grad_every_comp = against(grad_expanded, weight_expand)
    grad_comp, grad_rope_key = (
        lax.psum_scatter(
            grad_every_comp.astype(jnp.bfloat16), "ctx", scatter_dimension=0, tiled=True
        ).astype(jnp.float32),
        lax.psum_scatter(
            grad_keys_rope.astype(jnp.bfloat16), "ctx", scatter_dimension=0, tiled=True
        ).astype(jnp.float32),
    )
    grad_lat_comp, grad_lat_gain = norm_back(grad_comp, normed_lat, factor_lat, latent_gain)
    grad_latent = jnp.concatenate(
        [grad_lat_comp, rotate(grad_rope_key, cosine, -sine_part)], axis=1
    ).astype(jnp.bfloat16)
    grad_query = (
        jnp.concatenate(
            [grad_query_nope, rotate(grad_query_rope, cosine[:, None, :], -sine_part[:, None, :])],
            axis=-1,
        )
        .reshape(tok_count, -1)
        .astype(jnp.bfloat16)
    )
    grad_query_weight = across(hidden_one, grad_query)
    grad_latent_weight = across(hidden_one, grad_latent)
    grad_hidden_one = against(grad_query, weight_query) + against(grad_latent, weight_latent)
    grad_tokens, grad_attn = norm_back(grad_hidden_one, normed_one, factor_one, attn_gain)
    grad_inputs = (grad_first + grad_tokens).astype(jnp.bfloat16)[None]
    sliced = (
        lax.psum_scatter(
            grad_query_weight.astype(jnp.bfloat16), "expert", scatter_dimension=0, tiled=True
        ).astype(jnp.float32),
        lax.psum_scatter(
            grad_latent_weight.astype(jnp.bfloat16), "expert", scatter_dimension=0, tiled=True
        ).astype(jnp.float32),
        lax.psum_scatter(
            grad_expand_weight.astype(jnp.bfloat16), "expert", scatter_dimension=0, tiled=True
        ).astype(jnp.float32),
        lax.psum_scatter(
            grad_output_weight.astype(jnp.bfloat16), "expert", scatter_dimension=0, tiled=True
        ).astype(jnp.float32),
        lax.psum_scatter(
            grad_router_weight.astype(jnp.bfloat16), "expert", scatter_dimension=0, tiled=True
        ).astype(jnp.float32),
        lax.psum_scatter(
            grad_shared_in.astype(jnp.bfloat16), "expert", scatter_dimension=0, tiled=True
        ).astype(jnp.float32),
        lax.psum_scatter(
            grad_shared_out.astype(jnp.bfloat16), "expert", scatter_dimension=0, tiled=True
        ).astype(jnp.float32),
        lax.psum_scatter(
            grad_attn.astype(jnp.bfloat16), "expert", scatter_dimension=0, tiled=True
        ).astype(jnp.float32),
        lax.psum_scatter(
            grad_lat_gain.astype(jnp.bfloat16), "expert", scatter_dimension=0, tiled=True
        ).astype(jnp.float32),
        lax.psum_scatter(
            grad_ffn.astype(jnp.bfloat16), "expert", scatter_dimension=0, tiled=True
        ).astype(jnp.float32),
    )
    summed = (
        lax.psum(sliced[0].astype(jnp.bfloat16), ("dp", "ctx")).astype(jnp.float32),
        lax.psum(sliced[1].astype(jnp.bfloat16), ("dp", "ctx")).astype(jnp.float32),
        lax.psum(sliced[2].astype(jnp.bfloat16), ("dp", "ctx")).astype(jnp.float32),
        lax.psum(sliced[3].astype(jnp.bfloat16), ("dp", "ctx")).astype(jnp.float32),
        lax.psum(sliced[4].astype(jnp.bfloat16), ("dp", "ctx")).astype(jnp.float32),
        lax.psum(sliced[5].astype(jnp.bfloat16), ("dp", "ctx")).astype(jnp.float32),
        lax.psum(sliced[6].astype(jnp.bfloat16), ("dp", "ctx")).astype(jnp.float32),
        lax.psum(sliced[7].astype(jnp.bfloat16), ("dp", "ctx")).astype(jnp.float32),
        lax.psum(sliced[8].astype(jnp.bfloat16), ("dp", "ctx")).astype(jnp.float32),
        lax.psum(sliced[9].astype(jnp.bfloat16), ("dp", "ctx")).astype(jnp.float32),
    )
    return (
        output,
        grad_inputs,
        summed[7],
        summed[0],
        summed[1],
        summed[8],
        summed[2],
        summed[3],
        summed[9],
        summed[4],
        summed[5],
        summed[6],
        grad_weight_in,
        grad_weight_out,
    )


def solution(mesh):
    return jax.shard_map(
        body,
        mesh=mesh,
        in_specs=(
            P(("dp", "expert"), "ctx", None),
            P(("dp", "expert"), "ctx", None),
            P(("dp", "expert"), "ctx", None),
            P(),
            P("expert", None),
            P("expert", None),
            P(),
            P("expert", None),
            P("expert", None),
            P(),
            P("expert", None),
            P("expert", None),
            P("expert", None),
            P("expert", None, ("dp", "ctx"), None),
            P("expert", ("dp", "ctx"), None),
        ),
        out_specs=(
            P(("dp", "expert"), "ctx", None),
            P(("dp", "expert"), "ctx", None),
            P("expert"),
            P("expert", None),
            P("expert", None),
            P("expert"),
            P("expert", None),
            P("expert", None),
            P("expert"),
            P("expert", None),
            P("expert", None),
            P("expert", None),
            P("expert", None, ("dp", "ctx"), None),
            P("expert", ("dp", "ctx"), None),
        ),
        check_vma=False,
    )
```

profile of v0, /device:TPU:0, one launch (start us, length us, event | category | flops | bytes accessed | tf_op | source)
XLA Modules:
  0.0 2469.6 jit_solution(1711358386629692258)
XLA Ops:
  16.7 28.4 %all-gather.9.cloned.1.call-done = bf16[2048,576]{0,1:T(8,128)(2,1)} async-done(((bf16[256,576]{0,1:T(8,128)(2,1)}), bf16[2048,576]{0,1:T(8,128)(2,1)}) %all-gather.9.cloned.1.call-update) | async-done | bytes 2359312 | tf_op jit(solution)/shard_map/all_gather | solution.py:111
  55.6 36.8 %all-gather.11.cloned.1.call-done = bf16[512,4096]{1,0:T(8,128)(2,1)} async-done(((bf16[64,4096]{1,0:T(8,128)(2,1)}), bf16[512,4096]{1,0:T(8,128)(2,1)}) %all-gather.11.cloned.1.call-update) | async-done | bytes 4194320 | tf_op jit(solution)/shard_map/all_gather | solution.py:112
  100.8 108.8 %all-gather.13.cloned.1.call-done = bf16[2048,3072]{1,0:T(8,128)(2,1)} async-done(((bf16[256,3072]{1,0:T(8,128)(2,1)}), bf16[2048,3072]{1,0:T(8,128)(2,1)}) %all-gather.13.cloned.1.call-update) | async-done | bytes 12582928 | tf_op jit(solution)/shard_map/all_gather | solution.py:110
  209.5 16.3 copy.122
  238.5 52.7 %all-gather.15.cloned.1.call-done = bf16[2048,2048]{1,0:T(8,128)(2,1)} async-done(((bf16[256,2048]{1,0:T(8,128)(2,1)}), bf16[2048,2048]{1,0:T(8,128)(2,1)}) %all-gather.15.cloned.1.call-update) | async-done | bytes 8388624 | tf_op jit(solution)/shard_map/all_gather | solution.py:113
  304.1 97.6 %all_to_all.60 = bf16[8,2,64,2048]{3,2,1,0:T(8,128)(2,1)S(1)} all-to-all(bf16[8,2,64,2048]{3,2,1,0:T(8,128)(2,1)} %bitcast.221), channel_id=1, replica_groups=mesh['dp'=2,'ctx'=2,'expert'=8] {'expert'}, dimensions={0} | all-to-all | bytes 8388608 | tf_op jit(solution)/shard_map/all_to_all | solution.py:57
  420.4 14.5 all_gather.37
  453.0 97.6 %all_to_all.61 = bf16[8,2,64,2048]{3,2,1,0:T(8,128)(2,1)S(1)} all-to-all(bf16[8,2,64,2048]{3,2,1,0:T(8,128)(2,1)} %bitcast.222), channel_id=1, replica_groups=mesh['dp'=2,'ctx'=2,'expert'=8] {'expert'}, dimensions={0} | all-to-all | bytes 8388608 | tf_op jit(solution)/shard_map/all_to_all | solution.py:57
  560.4 19.9 fusion.2
  580.3 139.7 %all-gather.23.cloned.1.call-done = bf16[2,2048,2048]{2,1,0:T(8,128)(2,1)} async-done(((bf16[2,512,2048]{2,1,0:T(8,128)(2,1)}), bf16[2,2048,2048]{2,1,0:T(8,128)(2,1)}) %all-gather.23.cloned.1.call-update) | async-done | bytes 16777232 | tf_op jit(solution)/shard_map/all_gather | solution.py:65
  720.0 15.3 fusion.8
  735.3 20.5 bitcast_convert_fusion
  771.6 138.2 %reduce-scatter.18.cloned.1.call-done = bf16[2,512,2048]{2,1,0:T(8,128)(2,1)} async-done(((bf16[2,2048,2048]{2,1,0:T(8,128)(2,1)}), bf16[2,512,2048]{2,1,0:T(8,128)(2,1)}) %reduce-scatter.18.cloned.1.call-update) | async-done | bytes 4194320 | tf_op jit(solution)/shard_map/reduce_scatter | solution.py:69
  922.9 143.7 %reduce-scatter.16.cloned.1.call-done = bf16[2,512,2048]{2,1,0:T(8,128)(2,1)} async-done(((bf16[2,2048,2048]{2,1,0:T(8,128)(2,1)}), bf16[2,512,2048]{2,1,0:T(8,128)(2,1)}) %reduce-scatter.16.cloned.1.call-update) | async-done | bytes 4194320 | tf_op jit(solution)/shard_map/reduce_scatter | solution.py:69
  1080.1 280.3 %all-gather.17.cloned.1.call-done = bf16[2048,5632]{1,0:T(8,128)(2,1)} async-done(((bf16[256,5632]{1,0:T(8,128)(2,1)}), bf16[2048,5632]{1,0:T(8,128)(2,1)}) %all-gather.17.cloned.1.call-update) | async-done | bytes 23068688 | tf_op jit(solution)/shard_map/all_gather | solution.py:115
  1373.3 94.8 %all-gather.19.cloned.1.call-done = bf16[2816,2048]{1,0:T(8,128)(2,1)} async-done(((bf16[352,2048]{1,0:T(8,128)(2,1)}), bf16[2816,2048]{1,0:T(8,128)(2,1)}) %all-gather.19.cloned.1.call-update) | async-done | bytes 11534352 | tf_op jit(solution)/shard_map/all_gather | solution.py:116
  1624.4 89.6 %reduce-scatter.32.cloned.1.call-done = bf16[352,2048]{1,0:T(8,128)(2,1)} async-done(((bf16[2816,2048]{1,0:T(8,128)(2,1)}), bf16[352,2048]{1,0:T(8,128)(2,1)}) %reduce-scatter.32.cloned.1.call-update) | async-done | bytes 1441808 | tf_op jit(solution)/shard_map/reduce_scatter | solution.py:350
  1714.0 228.1 %reduce-scatter.30.cloned.1.call-done = bf16[256,5632]{1,0:T(8,128)(2,1)} async-done(((bf16[2048,5632]{1,0:T(8,128)(2,1)}), bf16[256,5632]{1,0:T(8,128)(2,1)}) %reduce-scatter.30.cloned.1.call-update) | async-done | bytes 2883600 | tf_op jit(solution)/shard_map/reduce_scatter | solution.py:347
  1942.1 38.4 %reduce-scatter.22.cloned.1.call-done = bf16[256,576]{0,1:T(8,128)(2,1)} async-done(((bf16[2048,576]{0,1:T(8,128)(2,1)}), bf16[256,576]{0,1:T(8,128)(2,1)}) %reduce-scatter.22.cloned.1.call-update) | async-done | bytes 294928 | tf_op jit(solution)/shard_map/reduce_scatter | solution.py:335
  1980.5 51.4 %reduce-scatter.24.cloned.1.call-done = bf16[64,4096]{1,0:T(8,128)(2,1)} async-done(((bf16[512,4096]{1,0:T(8,128)(2,1)}), bf16[64,4096]{1,0:T(8,128)(2,1)}) %reduce-scatter.24.cloned.1.call-update) | async-done | bytes 524304 | tf_op jit(solution)/shard_map/reduce_scatter | solution.py:338
  2031.9 90.1 %reduce-scatter.26.cloned.1.call-done = bf16[256,2048]{1,0:T(8,128)(2,1)} async-done(((bf16[2048,2048]{1,0:T(8,128)(2,1)}), bf16[256,2048]{1,0:T(8,128)(2,1)}) %reduce-scatter.26.cloned.1.call-update) | async-done | bytes 1048592 | tf_op jit(solution)/shard_map/reduce_scatter | solution.py:341
  2122.0 129.8 %reduce-scatter.20.cloned.1.call-done = bf16[256,3072]{1,0:T(8,128)(2,1)} async-done(((bf16[2048,3072]{1,0:T(8,128)(2,1)}), bf16[256,3072]{1,0:T(8,128)(2,1)}) %reduce-scatter.20.cloned.1.call-update) | async-done | bytes 1572880 | tf_op jit(solution)/shard_map/reduce_scatter | solution.py:332
  2268.7 19.5 fusion
  2337.0 112.7 %all-reduce.10.cloned.1.call-done = (bf16[256,3072]{1,0:T(8,128)(2,1)}, bf16[256,576]{0,1:T(8,128)(2,1)}, bf16[64,4096]{1,0:T(8,128)(2,1)}, bf16[256,2048]{1,0:T...) async-done(((bf16[256,3072]{1,0:T(8,128)(2,1)}, bf16[256,576]{0,1:T(8,128)(2,1)}, bf16[64,4096]{1,0:T(8,128)(2,1)}, bf16[256,2048]{1,0:T(8,128)(2,1)}, ...) | async-done | bytes 7766032 | tf_op jit(solution)/shard_map/psum | solution.py:364
  (347 shorter events, 387.9 us)
Async XLA Ops:
  7.2 712.8 %copy-start = (bf16[2,352,2048]{2,1,0:T(8,128)(2,1)S(1)}, bf16[2,352,2048]{2,1,0:T(8,128)(2,1)}, u32[]{:S(2)}) copy-start(bf16[2,352,2048]{2,1,0:T(8,128)(2,1)} %param.29) | copy-start | bytes 8650756
  7.2 37.9 %all-gather.9.cloned.1.call-start = ((), (), s32[]{:S(2)}) async-start(), calls=%async_computation.15 | async-start | bytes 2654208 | tf_op jit(solution)/shard_map/all_gather | solution.py:111
  8.0 84.4 %all-gather.11.cloned.1.call-start = ((), (), s32[]{:S(2)}) async-start(), calls=%async_computation.16 | async-start | bytes 4718592 | tf_op jit(solution)/shard_map/all_gather | solution.py:112
  8.7 200.8 %all-gather.13.cloned.1.call-start = ((), (), s32[]{:S(2)}) async-start(), calls=%async_computation.17 | async-start | bytes 14155776 | tf_op jit(solution)/shard_map/all_gather | solution.py:110
  9.5 281.8 %all-gather.15.cloned.1.call-start = ((), (), s32[]{:S(2)}) async-start(), calls=%async_computation.18 | async-start | bytes 9437184 | tf_op jit(solution)/shard_map/all_gather | solution.py:113
  10.0 550.3 %all-gather.21.cloned.1.call-start = ((), (), s32[]{:S(2)}) async-start(), calls=%async_computation.21 | async-start | bytes 20971520 | tf_op jit(solution)/shard_map/all_gather | solution.py:65
  404.1 315.9 %all-gather.23.cloned.1.call-start = ((), (), s32[]{:S(2)}) async-start(), calls=%async_computation.23 | async-start | bytes 20971520 | tf_op jit(solution)/shard_map/all_gather | solution.py:65
  552.9 356.9 %reduce-scatter.18.cloned.1.call-start = ((), (), s32[]{:S(2)}) async-start(), calls=%async_computation.24 | async-start | bytes 20971520 | tf_op jit(solution)/shard_map/reduce_scatter | solution.py:69
  755.9 310.7 %reduce-scatter.16.cloned.1.call-start = ((), (), s32[]{:S(2)}) async-start(), calls=%async_computation.22 | async-start | bytes 20971520 | tf_op jit(solution)/shard_map/reduce_scatter | solution.py:69
  770.3 590.1 %all-gather.17.cloned.1.call-start = ((), (), s32[]{:S(2)}) async-start(), calls=%async_computation.19 | async-start | bytes 25952256 | tf_op jit(solution)/shard_map/all_gather | solution.py:115
  771.0 697.1 %all-gather.19.cloned.1.call-start = ((), (), s32[]{:S(2)}) async-start(), calls=%async_computation.20 | async-start | bytes 12976128 | tf_op jit(solution)/shard_map/all_gather | solution.py:116
  918.3 156.8 %all-to-all-start.3 = ((bf16[1,2,512,2048]{3,1,0,2:T(2,128)(2,1)}), bf16[1,2,512,2048]{3,1,0,2:T(2,128)(2,1)}, u32[]{:S(2)}, u32[]{:S(2)}) async-start(bf16[1,2,512,2048]{3,1,0,2:T(2,128)(2,1)} %copy.138), calls=%async_computation.5 | async-start | bytes 8388608 | tf_op jit(solution)/shard_map/all_to_all | solution.py:61
  1075.1 438.9 %all-to-all-start.1 = ((bf16[1,2,512,2048]{3,1,0,2:T(2,128)(2,1)}), bf16[1,2,512,2048]{3,1,0,2:T(2,128)(2,1)}, u32[]{:S(2)}, u32[]{:S(2)}) async-start(bf16[1,2,512,2048]{3,1,0,2:T(2,128)(2,1)} %copy.133), calls=%async_computation.2 | async-start | bytes 8388608 | tf_op jit(solution)/shard_map/all_to_all | solution.py:61
  1080.0 514.2 %reduce-scatter.36.cloned.1.call-start = ((), (), s32[]{:S(2)}) async-start(), calls=%async_computation.33 | async-start | bytes 98304
  1080.1 388.0 %copy-start.27 = (bf16[1,128,2048]{2,1,0:T(8,128)(2,1)S(1)}, bf16[1,128,2048]{2,1,0:T(8,128)(2,1)}, u32[]{:S(2)}) copy-start(bf16[1,128,2048]{2,1,0:T(8,128)(2,1)} %param.16) | copy-start | bytes 1572868
  1569.0 26.2 %reduce-scatter.34.cloned.1.call-start = ((), (), s32[]{:S(2)}) async-start(), calls=%async_computation.32 | async-start | bytes 393216
  1573.9 140.1 %reduce-scatter.32.cloned.1.call-start = ((), (), s32[]{:S(2)}) async-start(), calls=%async_computation.31 | async-start | bytes 12976128 | tf_op jit(solution)/shard_map/reduce_scatter | solution.py:350
  1581.6 360.5 %reduce-scatter.30.cloned.1.call-start = ((), (), s32[]{:S(2)}) async-start(), calls=%async_computation.30 | async-start | bytes 25952256 | tf_op jit(solution)/shard_map/reduce_scatter | solution.py:347
  1594.0 386.5 %reduce-scatter.22.cloned.1.call-start = ((), (), s32[]{:S(2)}) async-start(), calls=%async_computation.26 | async-start | bytes 2654208 | tf_op jit(solution)/shard_map/reduce_scatter | solution.py:335
  1600.9 431.0 %reduce-scatter.24.cloned.1.call-start = ((), (), s32[]{:S(2)}) async-start(), calls=%async_computation.27 | async-start | bytes 4718592 | tf_op jit(solution)/shard_map/reduce_scatter | solution.py:338
  1605.3 516.7 %reduce-scatter.26.cloned.1.call-start = ((), (), s32[]{:S(2)}) async-start(), calls=%async_computation.28 | async-start | bytes 9437184 | tf_op jit(solution)/shard_map/reduce_scatter | solution.py:341
  1612.3 639.5 %reduce-scatter.20.cloned.1.call-start = ((), (), s32[]{:S(2)}) async-start(), calls=%async_computation.25 | async-start | bytes 14155776 | tf_op jit(solution)/shard_map/reduce_scatter | solution.py:332
  1623.5 698.0 %reduce-scatter.28.cloned.1.call-start = ((), (), s32[]{:S(2)}) async-start(), calls=%async_computation.29 | async-start | bytes 73728 | tf_op jit(solution)/shard_map/reduce_scatter | solution.py:344
  1624.4 825.3 %all-reduce.10.cloned.1.call-start = ((), (), s32[]{:S(2)}) async-start(), calls=%async_computation.34 | async-start | bytes 15532032 | tf_op jit(solution)/shard_map/psum | solution.py:364
  (82 other events, 1085.7 us)
Sparse Core Ops, SparseCore 0:
  9.6 35.4 all-gather.8
  46.7 45.6 all-gather.10
  94.0 115.5 all-gather.12
  211.0 80.2 all-gather.14
  404.2 156.1 all-gather.20
  562.6 157.2 all-gather.22
  756.0 153.7 reduce-scatter.17
  912.8 153.7 reduce-scatter.15
  1068.3 292.1 all-gather.16
  1361.9 106.1 all-gather.18
  1569.1 8.2 reduce-scatter.35
  1580.1 11.7 reduce-scatter.33
  1594.7 119.2 reduce-scatter.31
  1716.2 225.8 reduce-scatter.29
  1944.8 35.6 reduce-scatter.21
  1983.2 48.6 reduce-scatter.23
  2034.0 87.9 reduce-scatter.25
  2124.2 127.6 reduce-scatter.19
  2254.6 28.9 reduce-scatter.27
  2287.9 161.6 all-reduce.9
where the time goes:
time: 2480 us; the launch traced here: 2470 us
  waiting for transfers between devices  1770 us (71%)
  blocking collectives  242 us (10%)
  matrix products  240 us (10%)
  local copies, waits for them, and re-layouts  143 us (6%)
  other arithmetic  43.4 us (2%)
    reduce_scatter x2, waiting for transfers between devices, sum_rows(): lax.psum_scatter(partial_value.astype(jnp.bfloat16), ('dp', 'ctx'), scatt...  282 us
    all_gather x1, waiting for transfers between devices, body(): lax.all_gather(w_shared_in, 'expert', axis=0, tiled=True)  280 us
    reduce_scatter x1, waiting for transfers between devices, body(): lax.psum_scatter(grad_shared_in.astype(jnp.bfloat16), 'expert', scatter_d...  228 us
    all_to_all x2, blocking collectives, to_experts(): lax.all_to_all(buffer, 'expert', split_axis=0, concat_axis=2, tiled=True)  195 us
    all_gather x2, waiting for transfers between devices, share_rows(): return lax.all_gather(row_block, ('dp', 'ctx'), axis=1, tiled=True)  147 us
    reduce_scatter x1, waiting for transfers between devices, body(): lax.psum_scatter(grad_query_weight.astype(jnp.bfloat16), 'expert', scatte...  130 us
    psum x1, waiting for transfers between devices, body(): lax.psum(sliced[0].astype(jnp.bfloat16), ('dp', 'ctx')).astype(jnp.float32)  113 us
    all_gather x1, waiting for transfers between devices, body(): lax.all_gather(w_query, 'expert', axis=0, tiled=True)  109 us
  transfers between devices with their start and end apart: 22, of which 17 were waited for; matrix products, arithmetic and copies ran while one was open for 12% of the time, Pallas kernels for 0%

commit v1 on v0

--- a/solution.py
+++ b/solution.py
@@ -1,8 +1,11 @@
+import functools
 import math
 
 import jax
 import jax.numpy as jnp
 from jax import lax
+from jax.experimental import pallas as pl
+from jax.experimental.pallas import tpu as pltpu
 from jax.sharding import PartitionSpec as P
 
 HEADS = 16
@@ -15,6 +18,665 @@
 
 EPS = 1e-06
 
+MESH = pl.DeviceIdType.MESH
+ALL = ("dp", "ctx", "expert")
+PLANE = ("dp", "ctx")
+BF = jnp.bfloat16
+F32 = jnp.float32
+LANES = 128
+CHUNK = 512
+VMEM_LIMIT = 66_000_000
+
+
+def here():
+    spot = lax.axis_index("expert")
+    return lax.axis_index("dp"), lax.axis_index("ctx"), spot // 2, lax.rem(spot, 2)
+
+
+def greet(peers):
+    barrier = pltpu.get_barrier_semaphore()
+    for peer in peers:
+        pl.semaphore_signal(barrier, inc=1, device_id=peer, device_id_type=MESH)
+    pl.semaphore_wait(barrier, len(peers))
+
+
+class Sends:
+    def __init__(self, sems):
+        self.sems, self.started = sems, []
+
+    def go(self, src, dst, arrival, peer):
+        copy = pltpu.make_async_remote_copy(
+            src_ref=src,
+            dst_ref=dst,
+            send_sem=self.sems.at[len(self.started)],
+            recv_sem=arrival,
+            device_id=peer,
+            device_id_type=MESH,
+        )
+        copy.start()
+        self.started.append(copy)
+
+    def drain(self):
+        for copy in self.started:
+            copy.wait_send()
+
+
+def arrive(ref, sem, peer):
+    pltpu.make_async_remote_copy(
+        src_ref=ref, dst_ref=ref, send_sem=sem, recv_sem=sem, device_id=peer, device_id_type=MESH
+    ).wait_recv()
+
+
+def gather_all_kernel(nz, rows, own, out, lsem, ssem, zsem, xsem, ysem, dasem, dbsem, csem):
+    x, y, z, c = here()
+    half = rows // 2
+    first, second = pl.ds(0, half), pl.ds(half, half)
+    xn, yn, cn = (1 - x, y, 2 * z + c), (x, 1 - y, 2 * z + c), (x, y, 2 * z + 1 - c)
+    source = [lax.rem(z + nz - k, nz) for k in range(nz)]
+    zpeers = [(x, y, 2 * lax.rem(z + k, nz) + c) for k in range(1, nz)]
+    greet(zpeers + [xn, yn, cn])
+    sends = Sends(ssem)
+    mine = out.at[x, y, z, c]
+    for k in range(1, nz):
+        sends.go(own, mine, zsem.at[k], zpeers[k - 1])
+    local = pltpu.make_async_copy(own, mine, lsem)
+    local.start()
+
+    def column(j, src):
+        dst = out.at[x, y, source[j], c]
+        sends.go(src, dst, xsem.at[j], xn)
+        sends.go(src, dst, ysem.at[j], yn)
+        sends.go(src, dst, csem.at[j], cn)
+
+    def sides(j):
+        part = out.at[1 - x, y, source[j], c]
+        arrive(part, xsem.at[j], xn)
+        sends.go(part.at[first], part.at[first], dasem.at[j], yn)
+        sends.go(part, part, csem.at[nz + j], cn)
+        part = out.at[x, 1 - y, source[j], c]
+        arrive(part, ysem.at[j], yn)
+        sends.go(part.at[second], part.at[second], dbsem.at[j], xn)
+        sends.go(part, part, csem.at[2 * nz + j], cn)
+
+    def corner(j):
+        part = out.at[1 - x, 1 - y, source[j], c]
+        arrive(part.at[first], dasem.at[j], yn)
+        arrive(part.at[second], dbsem.at[j], xn)
+        sends.go(part, part, csem.at[3 * nz + j], cn)
+
+    column(0, own)
+    for step in range(1, nz + 2):
+        if step < nz:
+            part = out.at[x, y, source[step], c]
+            arrive(part, zsem.at[step], zpeers[0])
+            column(step, part)
+        if step - 1 < nz:
+            sides(step - 1)
+        if 0 <= step - 2 < nz:
+            corner(step - 2)
+    for q, (qx, qy) in enumerate(((x, y), (1 - x, y), (x, 1 - y), (1 - x, 1 - y))):
+        for j in range(nz):
+            arrive(out.at[qx, qy, source[j], 1 - c], csem.at[q * nz + j], cn)
+    sends.drain()
+    local.wait()
+
+
+def gather_all(own, nz, number):
+    rows, width = own.shape
+    dma = pltpu.SemaphoreType.DMA
+    return pl.pallas_call(
+        functools.partial(gather_all_kernel, nz, rows),
+        out_shape=jax.ShapeDtypeStruct((2, 2, nz, 2, rows, width), own.dtype),
+        in_specs=[pl.BlockSpec(memory_space=pltpu.VMEM)],
+        out_specs=pl.BlockSpec(memory_space=pl.ANY),
+        scratch_shapes=[
+            dma(()),
+            dma((9 * nz - 1,)),
+            dma((nz,)),
+            dma((nz,)),
+            dma((nz,)),
+            dma((nz,)),
+            dma((nz,)),
+            dma((4 * nz,)),
+        ],
+        compiler_params=pltpu.CompilerParams(collective_id=number, has_side_effects=True),
+        name=f"gather_all_{number}",
+    )(own)
+
+
+def sum_all_kernel(
+    nz, rows, part, out, own, rc, rda, rdb, rx, ry, rz, lsem, ssem, csem, dasem, dbsem, xsem, ysem, zsem
+):
+    x, y, z, c = here()
+    half = rows // 2
+    first, second = pl.ds(0, half), pl.ds(half, half)
+    xn, yn, cn = (1 - x, y, 2 * z + c), (x, 1 - y, 2 * z + c), (x, y, 2 * z + 1 - c)
+    dest = [lax.rem(z + 1 + i, nz) for i in range(nz)]
+    zpeers = [(x, y, 2 * dest[i] + c) for i in range(nz - 1)]
+    greet(zpeers + [xn, yn, cn])
+    sends = Sends(ssem)
+    quads = ((1 - x, 1 - y), (1 - x, y), (x, 1 - y), (x, y))
+    loads = {}
+    for i in range(nz):
+        for q, (qx, qy) in enumerate(quads):
+            sends.go(part.at[qx, qy, dest[i], 1 - c], rc.at[q, i], csem.at[q * nz + i], cn)
+            loads[q, i] = pltpu.make_async_copy(
+                part.at[qx, qy, dest[i], c], own.at[q, i], lsem.at[q * nz + i]
+            )
+            loads[q, i].start()
+
+    def base(q, i):
+        loads[q, i].wait()
+        arrive(rc.at[q, i], csem.at[q * nz + i], cn)
+
+    def val(ref):
+        return ref[...].astype(F32)
+
+    def corner(i):
+        base(0, i)
+        own[0, i] = (val(own.at[0, i]) + val(rc.at[0, i])).astype(BF)
+        sends.go(own.at[0, i, first], rda.at[i], dasem.at[i], yn)
+        sends.go(own.at[0, i, second], rdb.at[i], dbsem.at[i], xn)
+
+    def sides(i):
+        base(1, i)
+        own[1, i, second] = (val(own.at[1, i, second]) + val(rc.at[1, i, second])).astype(BF)
+        arrive(rda.at[i], dasem.at[i], yn)
+        own[1, i, first] = (
+            val(own.at[1, i, first]) + val(rc.at[1, i, first]) + val(rda.at[i])
+        ).astype(BF)
+        sends.go(own.at[1, i], rx.at[i], xsem.at[i], xn)
+        base(2, i)
+        own[2, i, first] = (val(own.at[2, i, first]) + val(rc.at[2, i, first])).astype(BF)
+        arrive(rdb.at[i], dbsem.at[i], xn)
+        own[2, i, second] = (
+            val(own.at[2, i, second]) + val(rc.at[2, i, second]) + val(rdb.at[i])
+        ).astype(BF)
+        sends.go(own.at[2, i], ry.at[i], ysem.at[i], yn)
+
+    def column(i):
+        base(3, i)
+        arrive(rx.at[i], xsem.at[i], xn)
+        arrive(ry.at[i], ysem.at[i], yn)
+        total = val(own.at[3, i]) + val(rc.at[3, i]) + val(rx.at[i]) + val(ry.at[i])
+        if i < nz - 1:
+            own[3, i] = total.astype(BF)
+            sends.go(own.at[3, i], rz.at[i], zsem.at[i], zpeers[i])
+        else:
+            for k in range(nz - 1):
+                arrive(rz.at[k], zsem.at[k], zpeers[0])
+                total = total + val(rz.at[k])
+            out[...] = total
+
+    for step in range(nz + 2):
+        if step < nz:
+            corner(step)
+        if 0 <= step - 1 < nz:
+            sides(step - 1)
+        if 0 <= step - 2 < nz:
+            column(step - 2)
+    sends.drain()
+
+
+def sum_all(part, nz, number):
+    rows, width = part.shape[-2:]
+    dma = pltpu.SemaphoreType.DMA
+
+    def space(*dims):
+        return pltpu.VMEM(dims + (width,), BF)
+
+    return pl.pallas_call(
+        functools.partial(sum_all_kernel, nz, rows),
+        out_shape=jax.ShapeDtypeStruct((rows, width), F32),
+        in_specs=[pl.BlockSpec(memory_space=pl.ANY)],
+        out_specs=pl.BlockSpec(memory_space=pltpu.VMEM),
+        scratch_shapes=[
+            space(4, nz, rows),
+            space(4, nz, rows),
+            space(nz, rows // 2),
+            space(nz, rows // 2),
+            space(nz, rows),
+            space(nz, rows),
+            space(nz - 1, rows),
+            dma((4 * nz,)),
+            dma((9 * nz - 1,)),
+            dma((4 * nz,)),
+            dma((nz,)),
+            dma((nz,)),
+            dma((nz,)),
+            dma((nz,)),
+            dma((nz - 1,)),
+        ],
+        compiler_params=pltpu.CompilerParams(
+            collective_id=number, has_side_effects=True, vmem_limit_bytes=VMEM_LIMIT
+        ),
+        name=f"sum_all_{number}",
+    )(part)
+
+
+def gather_plane_kernel(rows, own, out, lsem, ssem, rsem):
+    x, y, z, c = here()
+    half = rows // 2
+    first, second = pl.ds(0, half), pl.ds(half, half)
+    xn, yn = (1 - x, y, 2 * z + c), (x, 1 - y, 2 * z + c)
+    greet([xn, yn])
+    sends = Sends(ssem)
+    mine = out.at[x, y]
+    sends.go(own, mine, rsem.at[0], xn)
+    sends.go(own, mine, rsem.at[1], yn)
+    local = pltpu.make_async_copy(own, mine, lsem)
+    local.start()
+    part = out.at[1 - x, y]
+    arrive(part, rsem.at[0], xn)
+    sends.go(part.at[first], part.at[first], rsem.at[2], yn)
+    part = out.at[x, 1 - y]
+    arrive(part, rsem.at[1], yn)
+    sends.go(part.at[second], part.at[second], rsem.at[3], xn)
+    part = out.at[1 - x, 1 - y]
+    arrive(part.at[first], rsem.at[2], yn)
+    arrive(part.at[second], rsem.at[3], xn)
+    sends.drain()
+    local.wait()
+
+
+def gather_plane(own, number):
+    rows, width = own.shape
+    dma = pltpu.SemaphoreType.DMA
+    return pl.pallas_call(
+        functools.partial(gather_plane_kernel, rows),
+        out_shape=jax.ShapeDtypeStruct((2, 2, rows, width), own.dtype),
+        in_specs=[pl.BlockSpec(memory_space=pltpu.VMEM)],
+        out_specs=pl.BlockSpec(memory_space=pltpu.VMEM),
+        scratch_shapes=[dma(()), dma((4,)), dma((4,))],
+        compiler_params=pltpu.CompilerParams(collective_id=number, has_side_effects=True),
+        name=f"gather_plane_{number}",
+    )(own)
+
+
+def swap_plane_kernel(part, out, lsem, ssem, rsem):
+    x, y, z, c = here()
+    spots = ((1 - x, y), (x, 1 - y), (1 - x, 1 - y))
+    peers = [(px, py, 2 * z + c) for px, py in spots]
+    greet(peers)
+    sends = Sends(ssem)
+    for k, (px, py) in enumerate(spots):
+        sends.go(part.at[px, py], out.at[x, y], rsem.at[k], peers[k])
+    local = pltpu.make_async_copy(part.at[x, y], out.at[x, y], lsem)
+    local.start()
+    for k, (px, py) in enumerate(spots):
+        arrive(out.at[px, py], rsem.at[k], peers[k])
+    sends.drain()
+    local.wait()
+
+
+def swap_plane(part, number):
+    dma = pltpu.SemaphoreType.DMA
+    return pl.pallas_call(
+        swap_plane_kernel,
+        out_shape=jax.ShapeDtypeStruct(part.shape, part.dtype),
+        in_specs=[pl.BlockSpec(memory_space=pltpu.VMEM)],
+        out_specs=pl.BlockSpec(memory_space=pltpu.VMEM),
+        scratch_shapes=[dma(()), dma((3,)), dma((3,))],
+        compiler_params=pltpu.CompilerParams(collective_id=number, has_side_effects=True),
+        name=f"swap_plane_{number}",
+    )(part)
+
+
+def sum_plane_kernel(rows, part, out, rda, rdb, rx, ry, sx, sy, ssem, rsem):
+    x, y, z, c = here()
+    half = rows // 2
+    first, second = pl.ds(0, half), pl.ds(half, half)
+    xn, yn = (1 - x, y, 2 * z + c), (x, 1 - y, 2 * z + c)
+    greet([xn, yn])
+    sends = Sends(ssem)
+    corner, xside, yside = part.at[1 - x, 1 - y], part.at[1 - x, y], part.at[x, 1 - y]
+    sends.go(corner.at[first], rda, rsem.at[0], yn)
+    sends.go(corner.at[second], rdb, rsem.at[1], xn)
+    sends.go(xside.at[second], rx.at[second], rsem.at[2], xn)
+    sends.go(yside.at[first], ry.at[first], rsem.at[3], yn)
+    arrive(rda, rsem.at[0], yn)
+    sx[...] = (xside[first].astype(F32) + rda[...].astype(F32)).astype(BF)
+    sends.go(sx, rx.at[first], rsem.at[4], xn)
+    arrive(rdb, rsem.at[1], xn)
+    sy[...] = (yside[second].astype(F32) + rdb[...].astype(F32)).astype(BF)
+    sends.go(sy, ry.at[second], rsem.at[5], yn)
+    arrive(rx.at[second], rsem.at[2], xn)
+    arrive(ry.at[first], rsem.at[3], yn)
+    arrive(rx.at[first], rsem.at[4], xn)
+    arrive(ry.at[second], rsem.at[5], yn)
+    out[...] = part[x, y].astype(F32) + rx[...].astype(F32) + ry[...].astype(F32)
+    sends.drain()
+
+
+def sum_plane(part, number):
+    rows, width = part.shape[-2:]
+    dma = pltpu.SemaphoreType.DMA
+
+    def space(count):
+        return pltpu.VMEM((count, width), BF)
+
+    return pl.pallas_call(
+        functools.partial(sum_plane_kernel, rows),
+        out_shape=jax.ShapeDtypeStruct((rows, width), F32),
+        in_specs=[pl.BlockSpec(memory_space=pltpu.VMEM)],
+        out_specs=pl.BlockSpec(memory_space=pltpu.VMEM),
+        scratch_shapes=[
+            space(rows // 2),
+            space(rows // 2),
+            space(rows),
+            space(rows),
+            space(rows // 2),
+            space(rows // 2),
+            dma((6,)),
+            dma((6,)),
+        ],
+        compiler_params=pltpu.CompilerParams(collective_id=number, has_side_effects=True),
+        name=f"sum_plane_{number}",
+    )(part)
+
+
+def dot_nn(left, right):
+    return lax.dot_general(left, right, (((1,), (0,)), ((), ())), preferred_element_type=F32)
+
+
+def dot_nt(left, right):
+    return lax.dot_general(left, right, (((1,), (1,)), ((), ())), preferred_element_type=F32)
+
+
+def dot_tn(left, right):
+    return lax.dot_general(left, right, (((0,), (0,)), ((), ())), preferred_element_type=F32)
+
+
+def silu_parts(operand):
+    sigmoid_of = jax.nn.sigmoid(operand)
+    return (operand * sigmoid_of, sigmoid_of * (1.0 + operand * (1.0 - sigmoid_of)))
+
+
+def ffn_kernel(
+    dims,
+    h,
+    g,
+    pos,
+    win,
+    wout,
+    wcat,
+    wso,
+    out,
+    gh,
+    o_gwin,
+    o_gwout,
+    o_gwcat,
+    o_gwso,
+    rows,
+    grows,
+    gwin,
+    gwout,
+    gwcat,
+    gwso,
+    osem,
+):
+    hidden, padded, slots, shared, experts = dims
+    step = pl.program_id(0)
+    tokens, width = h.shape
+    block = 2 * LANES
+    pairs = tokens // block
+    per = 2 * slots
+    first_lane = shared + 2 * lax.axis_index("expert")
+
+    @pl.when(step == 0)
+    def _():
+        gwin[...] = jnp.zeros_like(gwin)
+        gwout[...] = jnp.zeros_like(gwout)
+        gwcat[...] = jnp.zeros_like(gwcat)
+        gwso[...] = jnp.zeros_like(gwso)
+
+    def chunks(body):
+        def run(n, carry):
+            body(pl.ds(pl.multiple_of(n * CHUNK, CHUNK), CHUNK))
+            return carry
+
+        lax.fori_loop(0, width // CHUNK, run, 0)
+
+    mixed = dot_nn(h[...], wcat[...])
+    gate, up = mixed[:, :LANES], mixed[:, LANES:]
+    lane = lax.broadcasted_iota(jnp.int32, gate.shape, 1)
+    of_router = (lane >= shared) & (lane < shared + experts)
+    logits = jnp.where(of_router, gate, -1e30)
+    raised = jnp.where(of_router, jnp.exp(logits - jnp.max(logits, axis=1, keepdims=True)), 0.0)
+    router = raised / jnp.sum(raised, axis=1, keepdims=True)
+    silu, slope = silu_parts(gate)
+    act = (silu * up).astype(BF)
+    gact = dot_nt(g[...], wso[...])
+    ggate = gact * up * slope
+    gup = gact * silu
+    high = router.astype(BF)
+    router_parts = jnp.concatenate([high, (router - high.astype(F32)).astype(BF)], axis=1)
+    slot_lane = lax.broadcasted_iota(jnp.int32, (per, LANES), 1)
+    slot_row = lax.broadcasted_iota(jnp.int32, (per, block), 0)
+    picks, picked = [], [[], []]
+    for pair in range(pairs):
+        span = slice(pair * block, (pair + 1) * block)
+        pick = jnp.concatenate(
+            [
+                jnp.where(pos[j : j + 1, span] == slot_row, 1.0, 0.0).astype(BF) for j in range(2)
+            ],
+            axis=0,
+        )
+        picks.append(pick)
+        place = slice(pair * per, (pair + 1) * per)
+
+        def fetch(cols, pick=pick, span=span, place=place):
+            taken = dot_nn(pick, h[span, cols]).astype(BF)
+            rows[0, place, cols] = taken[:per]
+            rows[1, place, cols] = taken[per:]
+            taken = dot_nn(pick, g[span, cols]).astype(BF)
+            grows[0, place, cols] = taken[:per]
+            grows[1, place, cols] = taken[per:]
+
+        chunks(fetch)
+        taken = dot_nn(pick, router_parts[span])
+        taken = taken[:, :LANES] + taken[:, LANES:]
+        for j in range(2):
+            picked[j].append(
+                jnp.sum(
+                    jnp.where(slot_lane == first_lane + j, taken[j * per : (j + 1) * per], 0.0),
+                    axis=1,
+                    keepdims=True,
+                )
+            )
+    grad_picked = []
+    for j in range(2):
+        share = jnp.concatenate(picked[j], axis=0)
+        both = dot_nt(rows[j], win[j])
+        egate, eup = both[:, :padded], both[:, padded:]
+        raw = dot_nt(grows[j], wout[j])
+        esilu, eslope = silu_parts(egate)
+        eact = esilu * eup
+        grad_picked.append(jnp.sum(eact * raw, axis=1, keepdims=True))
+        scaled = (share * eact).astype(BF)
+        graw = share * raw
+        gboth = jnp.concatenate([graw * eup * eslope, graw * esilu], axis=1).astype(BF)
+
+        def expert(cols, j=j, scaled=scaled, gboth=gboth):
+            gin, gout = rows[j, :, cols], grows[j, :, cols]
+            gwout[j, :, cols] += dot_tn(scaled[:, :hidden], gout)
+            gwin[j, 0, :, cols] += dot_tn(gboth[:, :hidden], gin)
+            gwin[j, 1, :, cols] += dot_tn(gboth[:, padded : padded + hidden], gin)
+            grows[j, :, cols] = dot_nn(scaled, wout[j, :, cols]).astype(BF)
+            rows[j, :, cols] = dot_nn(gboth, win[j, :, cols]).astype(BF)
+
+        chunks(expert)
+    gparts = []
+    for pair in range(pairs):
+        span = slice(pair * block, (pair + 1) * block)
+        place = slice(pair * per, (pair + 1) * per)
+        pick = picks[pair]
+        spread = jnp.concatenate(
+            [
+                jnp.where(slot_lane == first_lane + j, grad_picked[j][place], 0.0)
+                for j in range(2)
+            ],
+            axis=0,
+        )
+        high = spread.astype(BF)
+        low = (spread - high.astype(F32)).astype(BF)
+        grouter = dot_tn(pick, jnp.concatenate([high, low], axis=1))
+        grouter = grouter[:, :LANES] + grouter[:, LANES:]
+        share = router[span]
+        glogits = share * (grouter - jnp.sum(share * grouter, axis=1, keepdims=True))
+        gpart = jnp.concatenate([ggate[span] + glogits, gup[span]], axis=1).astype(BF)
+        gparts.append(gpart)
+
+        def spreads(cols, pick=pick, span=span, place=place, gpart=gpart):
+            sent = jnp.concatenate([grows[0, place, cols], grows[1, place, cols]], axis=0)
+            out[span, cols] = (dot_tn(pick, sent) + dot_nn(act[span], wso[:, cols])).astype(BF)
+            sent = jnp.concatenate([rows[0, place, cols], rows[1, place, cols]], axis=0)
+            gh[span, cols] = (dot_tn(pick, sent) + dot_nt(gpart, wcat[cols, :])).astype(BF)
+
+        chunks(spreads)
+    gall = jnp.concatenate(gparts, axis=0)
+
+    def dense(cols):
+        gwcat[:, cols] += dot_tn(gall, h[:, cols])
+        gwso[:, cols] += dot_tn(act, g[:, cols])
+
+    chunks(dense)
+
+    @pl.when(step == pl.num_programs(0) - 1)
+    def _():
+        copies = [
+            pltpu.make_async_copy(src, dst, osem.at[k])
+            for k, (src, dst) in enumerate(
+                ((gwin, o_gwin), (gwout, o_gwout), (gwcat, o_gwcat), (gwso, o_gwso))
+            )
+        ]
+        for copy in copies:
+            copy.start()
+        for copy in copies:
+            copy.wait()
+
+
+def ffn(h, g, pos, win, wout, wcat, wso, hidden, slots, shared, experts):
+    count, width = h.shape
+    padded = wout.shape[1]
+    tokens = 4 * LANES
+    whole = pl.Buffered(1)
+
+    def fixed(shape):
+        return pl.BlockSpec(shape, lambda i: (0,) * len(shape), pipeline_mode=whole)
+
+    moving = pl.BlockSpec((tokens, width), lambda i: (i, 0))
+    left = pl.BlockSpec(memory_space=pl.ANY)
+    sums = [(2, 2, hidden, width), (2, hidden, width), (2 * LANES, width), (LANES, width)]
+    return pl.pallas_call(
+        functools.partial(ffn_kernel, (hidden, padded, slots, shared, experts)),
+        grid=(count // tokens,),
+        out_shape=[jax.ShapeDtypeStruct((count, width), BF)] * 2
+        + [jax.ShapeDtypeStruct(s, F32) for s in sums],
+        in_specs=[
+            moving,
+            moving,
+            pl.BlockSpec((8, tokens), lambda i: (0, i)),
+            fixed(win.shape),
+            fixed(wout.shape),
+            fixed(wcat.shape),
+            fixed(wso.shape),
+        ],
+        out_specs=[moving, moving, left, left, left, left],
+        scratch_shapes=[
+            pltpu.VMEM((2, tokens // LANES * slots, width), BF),
+            pltpu.VMEM((2, tokens // LANES * slots, width), BF),
+        ]
+        + [pltpu.VMEM(s, F32) for s in sums]
+        + [pltpu.SemaphoreType.DMA((4,))],
+        compiler_params=pltpu.CompilerParams(vmem_limit_bytes=VMEM_LIMIT),
+        name="ffn",
+    )(h, g, pos, win, wout, wcat, wso)
+
+
+def head_parts(qn, qf, qs, ex, kf, ks):
+    lane = lax.broadcasted_iota(jnp.int32, qf.shape, 1)
+    low = pl.program_id(1) * (ROPE // 2)
+    mine = (lane >= low) & (lane < low + ROPE // 2)
+    zero = jnp.zeros_like(qf[...])
+    left = jnp.concatenate(
+        [qn[...], jnp.where(mine, qf[...], zero), jnp.where(mine, qs[...], zero)], axis=1
+    )
+    right = jnp.concatenate([ex[:, :NOPE], kf[...], ks[...]], axis=1)
+    scores = dot_nt(left, right) * (1.0 / math.sqrt(NOPE + ROPE))
+    row = lax.broadcasted_iota(jnp.int32, scores.shape, 0)
+    col = lax.broadcasted_iota(jnp.int32, scores.shape, 1)
+    scores = jnp.where(col <= row, scores, -1e30)
+    exponent = jnp.exp(scores - jnp.max(scores, axis=1, keepdims=True))
+    probs = exponent / jnp.sum(exponent, axis=1, keepdims=True)
+    return left, right, probs, mine
+
+
+def attend_kernel(qn, qf, qs, ex, kf, ks, mixed):
+    probs = head_parts(qn, qf, qs, ex, kf, ks)[2]
+    mixed[...] = dot_nn(probs.astype(BF), ex[:, NOPE:]).astype(BF)
+
+
+def attend_back_kernel(qn, qf, qs, ex, kf, ks, gm, gqn, gqf, gqs, gex, gkf, gks):
+    left, right, probs, mine = head_parts(qn, qf, qs, ex, kf, ks)
+    scale = 1.0 / math.sqrt(NOPE + ROPE)
+
+    @pl.when(pl.program_id(1) == 0)
+    def _():
+        for ref in (gqf, gqs, gkf, gks):
+            ref[...] = jnp.zeros_like(ref)
+
+    gweights = dot_nt(gm[...], ex[:, NOPE:])
+    gscores = probs * (gweights - jnp.sum(probs * gweights, axis=1, keepdims=True))
+    gscores = gscores.astype(BF)
+    gleft = dot_nn(gscores, right) * scale
+    gqn[...] = gleft[:, :NOPE].astype(BF)
+    gqf[...] += jnp.where(mine, gleft[:, NOPE : NOPE + LANES], 0.0)
+    gqs[...] += jnp.where(mine, gleft[:, NOPE + LANES :], 0.0)
+    gright = dot_tn(gscores, left) * scale
+    gex[:, :NOPE] = gright[:, :NOPE].astype(BF)
+    gkf[...] += gright[:, NOPE : NOPE + LANES]
+    gks[...] += gright[:, NOPE + LANES :]
+    gex[:, NOPE:] = dot_tn(probs.astype(BF), gm[...]).astype(BF)
+
+
+def attention_specs(length):
+    each = pl.BlockSpec((length, NOPE), lambda b, h: (b, h))
+    one = pl.BlockSpec((length, LANES), lambda b, h: (b, 0))
+    wide = pl.BlockSpec((length, NOPE + VH), lambda b, h: (b, h))
+    return each, one, wide
+
+
+def attend(qn, qf, qs, ex, kf, ks, length):
+    each, one, wide = attention_specs(length)
+    return pl.pallas_call(
+        attend_kernel,
+        grid=(qn.shape[0] // length, qn.shape[1] // NOPE),
+        out_shape=jax.ShapeDtypeStruct(qn.shape, BF),
+        in_specs=[each, one, one, wide, one, one],
+        out_specs=each,
+        name="attend",
+    )(qn, qf, qs, ex, kf, ks)
+
+
+def attend_back(qn, qf, qs, ex, kf, ks, gm, length):
+    each, one, wide = attention_specs(length)
+    return pl.pallas_call(
+        attend_back_kernel,
+        grid=(qn.shape[0] // length, qn.shape[1] // NOPE),
+        out_shape=[
+            jax.ShapeDtypeStruct(qn.shape, BF),
+            jax.ShapeDtypeStruct(qf.shape, F32),
+            jax.ShapeDtypeStruct(qf.shape, F32),
+            jax.ShapeDtypeStruct(ex.shape, BF),
+            jax.ShapeDtypeStruct(qf.shape, F32),
+            jax.ShapeDtypeStruct(qf.shape, F32),
+        ],
+        in_specs=[each, one, one, wide, one, one, each],
+        out_specs=[each, one, one, wide, one, one],
+        name="attend_back",
+    )(qn, qf, qs, ex, kf, ks, gm)
+
 
 def normalize(operand):
     factor = lax.rsqrt(jnp.mean(operand * operand, axis=-1, keepdims=True) + EPS)
@@ -25,6 +687,271 @@
     inner_sums = grad_out * gain_row
     grad_in = factor * (inner_sums - normed * jnp.mean(inner_sums * normed, axis=-1, keepdims=True))
     return (grad_in, jnp.sum(grad_out * normed, axis=0))
+
+
+def plane_part(operand, index, axis, parts=4):
+    size = operand.shape[axis] // parts
+    return lax.dynamic_slice_in_dim(operand, index * size, size, axis=axis)
+
+
+def columns_of(blocks):
+    return jnp.moveaxis(blocks, 0, 1).reshape(blocks.shape[1], -1)
+
+
+def split_body(
+    layer_input,
+    cotangent,
+    routes,
+    attn_gain,
+    w_query,
+    w_latent,
+    latent_gain,
+    w_expand,
+    w_output,
+    ffn_gain,
+    w_router,
+    w_shared_in,
+    w_shared_out,
+    w_expert_in,
+    w_expert_out,
+):
+    spot = lax.axis_index("expert")
+    place = lax.axis_index("dp") * 2 + lax.axis_index("ctx")
+    groups = lax.axis_size("expert")
+    nz = groups // 2
+    tok_count, width = layer_input.shape[1:]
+    length = 2 * tok_count
+    devices = 4 * groups
+    experts = w_router.shape[1]
+    capacity = tok_count * TOP * 4 // (3 * experts)
+    local_rows = w_query.shape[0]
+    heads = HEADS // 4
+    nope_cols, rope_cols = heads * NOPE, heads * ROPE // 2
+    query_cols = nope_cols + 2 * rope_cols
+    out_cols = width // 4
+    hidden = w_expert_out.shape[1]
+    padded = -(-hidden // LANES) * LANES
+    shared_rows = w_shared_out.shape[0]
+    units = shared_rows // 4
+
+    tokens = layer_input[0].astype(F32)
+    normed_one, factor_one = normalize(tokens)
+    hidden_one = (normed_one * attn_gain).astype(BF)
+    h1 = gather_plane(hidden_one, 1).reshape(4 * tok_count, width)
+    own_query = plane_part(w_query, place, 1).reshape(local_rows, heads, NOPE + ROPE)
+    half = NOPE + ROPE // 2
+    attn_pack = jnp.concatenate(
+        [
+            own_query[:, :, :NOPE].reshape(local_rows, nope_cols),
+            own_query[:, :, NOPE:half].reshape(local_rows, rope_cols),
+            own_query[:, :, half:].reshape(local_rows, rope_cols),
+            plane_part(w_output, place, 1),
+            w_latent,
+        ],
+        axis=1,
+    )
+    attn_w = lax.all_gather(attn_pack, "expert", axis=0, tiled=True)
+    weight_expand = lax.all_gather(plane_part(w_expand, place, 1), "expert", axis=0, tiled=True)
+    weight_query = attn_w[:, :query_cols]
+    weight_output = attn_w[:, query_cols : query_cols + out_cols].reshape(4, out_cols, out_cols)
+    weight_latent = attn_w[:, query_cols + out_cols :]
+
+    all_routes = lax.all_gather(routes[0], ALL, axis=0)
+    all_grads = lax.all_gather(cotangent[0], ALL, axis=0, tiled=True)
+    offset = (jnp.arange(devices, dtype=jnp.int32) % 2 * capacity)[:, None]
+    slots = []
+    for j in range(2):
+        named = jnp.any(all_routes == 2 * spot + j, axis=2)
+        order = jnp.cumsum(named.astype(jnp.int32), axis=1) - 1
+        slots.append(jnp.where(named, order + offset, -1).reshape(1, -1))
+    slots = jnp.concatenate(slots + [jnp.full((6, slots[0].shape[1]), -1, jnp.int32)], axis=0)
+    halves = w_shared_in.reshape(local_rows, 2, groups, 4, units)
+    halves = lax.dynamic_index_in_dim(halves, place, axis=3, keepdims=False)
+    spare = LANES - units - experts
+    shared_pack = jnp.concatenate(
+        [
+            halves[:, 0],
+            jnp.broadcast_to(w_router[:, None, :], (local_rows, groups, experts)),
+            jnp.zeros((local_rows, groups, spare), BF),
+            halves[:, 1],
+            jnp.zeros((local_rows, groups, LANES - units), BF),
+        ],
+        axis=2,
+    )
+    weight_shared = lax.all_to_all(
+        jnp.moveaxis(shared_pack, 1, 0), "expert", split_axis=0, concat_axis=0, tiled=True
+    ).reshape(width, 2 * LANES)
+    own_shared_out = jnp.pad(plane_part(w_shared_out, place, 0), ((0, LANES - units), (0, 0)))
+    widen = padded - hidden
+    expert_in = jnp.pad(w_expert_in, ((0, 0), (0, 0), (0, widen), (0, 0))).reshape(
+        2, 2 * padded, width
+    )
+    expert_down = jnp.pad(w_expert_out, ((0, 0), (0, widen), (0, 0)))
+
+    inverse = 10000.0 ** (-jnp.arange(0, ROPE, 2).astype(F32) / ROPE)
+    places = jnp.arange(4 * tok_count, dtype=jnp.int32) % length
+    angles = places.astype(F32)[:, None] * inverse[None, :]
+    cosine, sine_part = jnp.cos(angles), jnp.sin(angles)
+    cosines, sines = jnp.tile(cosine, (1, heads)), jnp.tile(sine_part, (1, heads))
+    queries = dot_nn(h1, weight_query)
+    query_nope = queries[:, :nope_cols].astype(BF)
+    former = queries[:, nope_cols : nope_cols + rope_cols]
+    latter = queries[:, nope_cols + rope_cols :]
+    query_f = (former * cosines - latter * sines).astype(BF)
+    query_s = (latter * cosines + former * sines).astype(BF)
+    latent = dot_nn(h1, weight_latent)
+    normed_lat, factor_lat = normalize(latent[:, :KV])
+    compressed = (normed_lat * latent_gain).astype(BF)
+    former, latter = latent[:, KV : KV + ROPE // 2], latent[:, KV + ROPE // 2 :]
+    key_f = jnp.tile((former * cosine - latter * sine_part).astype(BF), (1, heads))
+    key_s = jnp.tile((latter * cosine + former * sine_part).astype(BF), (1, heads))
+    expanded = dot_nn(compressed, weight_expand).astype(BF)
+    mixed = attend(query_nope, query_f, query_s, expanded, key_f, key_s, length)
+    mixed = gather_plane(mixed, 2).reshape(4, 4 * tok_count, nope_cols)
+    part = jnp.einsum("ptk,pkn->tn", mixed, weight_output, preferred_element_type=F32)
+    part = swap_plane(part.astype(BF).reshape(2, 2, tok_count, out_cols), 3)
+    first_sum = tokens + columns_of(part.reshape(4, tok_count, out_cols)).astype(F32)
+
+    normed_two, factor_two = normalize(first_sum)
+    hidden_two = (normed_two * ffn_gain).astype(BF)
+    h2 = gather_all(hidden_two, nz, 4).reshape(devices * tok_count, width)
+    out_part, back_part, grad_in, grad_down, grad_cat, grad_so = ffn(
+        h2,
+        all_grads,
+        slots,
+        expert_in,
+        expert_down,
+        weight_shared,
+        own_shared_out,
+        hidden,
+        capacity,
+        units,
+        experts,
+    )
+    spread = (2, 2, nz, 2, tok_count, width)
+    grad_h2 = sum_all(back_part.reshape(spread), nz, 5)
+    ffn_out = sum_all(out_part.reshape(spread), nz, 6)
+    output = (first_sum + ffn_out).astype(BF)[None]
+    grad_out = cotangent[0].astype(F32)
+    grad_norm, grad_ffn = norm_back(grad_h2, normed_two, factor_two, ffn_gain)
+    grad_first = grad_out + grad_norm
+
+    low = jnp.moveaxis(grad_first.astype(BF).reshape(tok_count, 4, out_cols), 1, 0)
+    low = swap_plane(low.reshape(2, 2, tok_count, out_cols), 7).reshape(-1, out_cols)
+    grad_mixed = jnp.einsum("tn,pkn->ptk", low, weight_output, preferred_element_type=F32)
+    grad_mixed = sum_plane(grad_mixed.astype(BF).reshape(2, 2, 4 * tok_count, nope_cols), 8)
+    grad_wo = jnp.einsum("ptk,tn->pkn", mixed, low, preferred_element_type=F32)
+    gqn, gqf, gqs, gex, gkf, gks = attend_back(
+        query_nope, query_f, query_s, expanded, key_f, key_s, grad_mixed.astype(BF), length
+    )
+    grad_comp = dot_nt(gex, weight_expand)
+    grad_we = dot_tn(compressed, gex)
+    lat_cols = KV + ROPE
+    lat_pad = -(-lat_cols // LANES) * LANES - lat_cols
+    grad_lat = jnp.concatenate(
+        [
+            grad_comp,
+            jnp.sum(gkf.reshape(-1, heads, ROPE // 2), axis=1),
+            jnp.sum(gks.reshape(-1, heads, ROPE // 2), axis=1),
+            jnp.zeros((4 * tok_count, lat_pad), F32),
+        ],
+        axis=1,
+    ).astype(BF)
+    grad_lat = sum_plane(grad_lat.reshape(2, 2, tok_count, -1), 9)
+
+    def own_rows(operand):
+        return lax.dynamic_slice_in_dim(operand, place * tok_count, tok_count, axis=0)
+
+    grad_lat_in, grad_lat_gain = norm_back(
+        grad_lat[:, :KV], own_rows(normed_lat), own_rows(factor_lat), latent_gain
+    )
+    own_cos, own_sin = own_rows(cosine), own_rows(sine_part)
+    former, latter = grad_lat[:, KV : KV + ROPE // 2], grad_lat[:, KV + ROPE // 2 : lat_cols]
+    own_latent = jnp.concatenate(
+        [
+            grad_lat_in,
+            former * own_cos + latter * own_sin,
+            latter * own_cos - former * own_sin,
+            jnp.zeros((tok_count, lat_pad), F32),
+        ],
+        axis=1,
+    ).astype(BF)
+    grad_latent = gather_plane(own_latent, 10).reshape(4 * tok_count, -1)[:, :lat_cols]
+    grad_query = jnp.concatenate(
+        [
+            gqn,
+            (gqf * cosines + gqs * sines).astype(BF),
+            (gqs * cosines - gqf * sines).astype(BF),
+        ],
+        axis=1,
+    )
+    grad_wq = dot_tn(h1, grad_query)
+    grad_wl = dot_tn(h1, plane_part(grad_latent, place, 1))
+    grad_h1 = dot_nt(grad_query, weight_query).astype(BF)
+    grad_h1 = sum_plane(grad_h1.reshape(2, 2, tok_count, width), 11)
+    grad_h1 = grad_h1 + dot_nt(own_latent[:, :lat_cols], weight_latent)
+    grad_tokens, grad_attn = norm_back(grad_h1, normed_one, factor_one, attn_gain)
+    grad_inputs = (grad_first + grad_tokens).astype(BF)[None]
+
+    grads = jnp.concatenate(
+        [grad_wq.astype(BF), grad_wo.reshape(width, out_cols).astype(BF), grad_wl.astype(BF)],
+        axis=1,
+    )
+    grads = lax.psum_scatter(grads, "expert", scatter_dimension=0, tiled=True)
+    grads = lax.all_gather(grads, PLANE, axis=0)
+    grad_we = lax.psum_scatter(grad_we.astype(BF), "expert", scatter_dimension=0, tiled=True)
+    grad_we = lax.all_gather(grad_we, PLANE, axis=1, tiled=True).astype(F32)
+    grad_wq = jnp.concatenate(
+        [
+            grads[:, :, :nope_cols].reshape(4, local_rows, heads, NOPE),
+            grads[:, :, nope_cols : nope_cols + rope_cols].reshape(4, local_rows, heads, -1),
+            grads[:, :, nope_cols + rope_cols : query_cols].reshape(4, local_rows, heads, -1),
+        ],
+        axis=3,
+    )
+    grad_wq = columns_of(grad_wq.reshape(4, local_rows, -1)).astype(F32)
+    grad_wo = columns_of(grads[:, :, query_cols : query_cols + out_cols]).astype(F32)
+    grad_wl = columns_of(grads[:, :, query_cols + out_cols :]).astype(F32)
+    shared_in = jnp.concatenate([grad_cat[:units], grad_cat[LANES : LANES + units]], axis=0)
+    shared_in = lax.all_to_all(
+        shared_in.astype(BF).reshape(2 * units, groups, local_rows),
+        "expert",
+        split_axis=1,
+        concat_axis=0,
+        tiled=True,
+    )
+    shared_in = lax.all_gather(shared_in.reshape(-1, local_rows), PLANE, axis=0)
+    shared_in = shared_in.reshape(4, groups, 2, units, local_rows)
+    shared_in = shared_in.transpose(4, 2, 1, 0, 3).reshape(local_rows, -1).astype(F32)
+    shared_out = lax.all_gather(grad_so[:units].astype(BF), PLANE, axis=0, tiled=True).astype(F32)
+    small = jnp.concatenate(
+        [
+            grad_cat[units : units + experts],
+            grad_attn[None],
+            grad_ffn[None],
+            jnp.pad(grad_lat_gain, (0, width - KV))[None],
+        ],
+        axis=0,
+    )
+    small = lax.psum(small, ALL)
+    rows = plane_part(small, spot, 1, groups)
+    lat_rows = plane_part(small[experts + 2, :KV], spot, 0, groups)
+    return (
+        output,
+        grad_inputs,
+        rows[experts],
+        grad_wq,
+        grad_wl,
+        lat_rows,
+        grad_we,
+        grad_wo,
+        rows[experts + 1],
+        rows[:experts].T,
+        shared_in,
+        shared_out,
+        grad_in,
+        grad_down,
+    )
 
 
 def rotate(operand, cosine, sine_part):
@@ -48,11 +975,6 @@
     )
 
 
-def silu_parts(operand):
-    sigmoid_of = jax.nn.sigmoid(operand)
-    return (operand * sigmoid_of, sigmoid_of * (1.0 + operand * (1.0 - sigmoid_of)))
-
-
 def to_experts(buffer):
     return lax.all_to_all(buffer, "expert", split_axis=0, concat_axis=2, tiled=True)
 
@@ -81,7 +1003,7 @@
     return jnp.where(allowed[None], scores * scale_factor, -1e30)
 
 
-def body(
+def general_body(
     layer_input,
     cotangent,
     routes,
@@ -391,8 +1313,9 @@
 
 
 def solution(mesh):
+    dense = mesh.shape["dp"] == 2 and mesh.shape["ctx"] == 2 and mesh.shape["expert"] == 8
     return jax.shard_map(
-        body,
+        split_body if dense else general_body,
         mesh=mesh,
         in_specs=(
             P(("dp", "expert"), "ctx", None),

time: 2480 us -> 1130 us (0.46)
  waiting for transfers between devices: 1770 us -> 189 us
  Pallas kernels: 0 us -> 602 us
  matrix products: 240 us -> 39.9 us
  blocking collectives: 242 us -> 136 us
  local copies, waits for them, and re-layouts: 143 us -> 89.1 us
    reduce_scatter x9 -> x2, waiting for transfers between devices: 909 us -> 37.7 us  [the longest x1 32.2 us: split_body(): lax.psum_scatter(grad_we.astype(BF), 'expert', scatter_dimension=0, tiled...]
    all_gather x8 -> x6, waiting for transfers between devices: 749 us -> 90.9 us  [the longest x1 40.3 us: split_body(): shared_in = lax.all_gather(shared_in.reshape(-1, local_rows), PLANE, axis=0)]
    pallas_call x0 -> x14, Pallas kernels: none -> 602 us  [the longest x2 182 us: sum_all(): pl.pallas_call(functools.partial(sum_all_kernel, nz, rows), out_shape=jax...]
    dot_general x36 -> x12, matrix products: 240 us -> 39.9 us  [the longest x3 10.8 us: dot_nt(): lax.dot_general(left, right, (((1,), (1,)), ((), ())), preferred_element_...]
    all_to_all x2 -> x1, blocking collectives: 195 us -> 34.6 us  [split_body(): lax.all_to_all(shared_in.astype(BF).reshape(2 * units, groups, local_rows...]
    all_gather x2, blocking collectives: 21.5 us -> 102 us  [the longest x1 91.6 us: split_body(): all_routes = lax.all_gather(routes[0], ALL, axis=0)]
    psum x1, waiting for transfers between devices: 113 us -> 59.8 us  [split_body(): small = lax.psum(small, ALL)]
    gather x4 -> x0, local copies, waits for them, and re-layouts: 36.7 us -> none  [the longest x1 11.1 us: body(): jnp.concatenate([sending, jnp.zeros((1, row_width), jnp.bfloat16)], axis=0)]
  transfers between devices with their start and end apart: 22 -> 10, of which waited for: 17 -> 6; matrix products, arithmetic and copies ran while one was open for 12% -> 9% of each run, Pallas kernels for 0% -> 24%
where the time goes in v1:
time: 1130 us; the launch traced here: 1120 us
  Pallas kernels  602 us (53%)
  waiting for transfers between devices  189 us (17%)
  blocking collectives  136 us (12%)
  local copies, waits for them, and re-layouts  89.1 us (8%)
  other arithmetic  42 us (4%)
  matrix products  39.9 us (4%)
  between operations  15.2 us (1%)
    pallas_call x2, Pallas kernels, sum_all(): pl.pallas_call(functools.partial(sum_all_kernel, nz, rows), out_shape=jax...  182 us
    pallas_call x1, Pallas kernels, ffn(): pl.pallas_call(functools.partial(ffn_kernel, (hidden, padded, slots, shar...  176 us
    all_gather x1, blocking collectives, split_body(): all_routes = lax.all_gather(routes[0], ALL, axis=0)  91.6 us
    pallas_call x1, Pallas kernels, gather_all(): pl.pallas_call(functools.partial(gather_all_kernel, nz, rows), out_shape=...  86.3 us
    pallas_call x3, Pallas kernels, gather_plane(): pl.pallas_call(functools.partial(gather_plane_kernel, rows), out_shape=ja...  61.9 us
    psum x1, waiting for transfers between devices, split_body(): small = lax.psum(small, ALL)  59.8 us
    pallas_call x3, Pallas kernels, sum_plane(): pl.pallas_call(functools.partial(sum_plane_kernel, rows), out_shape=jax.S...  49.9 us
    all_gather x1, waiting for transfers between devices, split_body(): shared_in = lax.all_gather(shared_in.reshape(-1, local_rows), PLANE, axis=0)  40.3 us
  transfers between devices with their start and end apart: 10, of which 6 were waited for; matrix products, arithmetic and copies ran while one was open for 9% of the time, Pallas kernels for 24%

profile of v1, /device:TPU:0, one launch (start us, length us, event | category | flops | bytes accessed | tf_op | source)
XLA Modules:
  0.0 1121.0 jit_solution(1386907592199786823)
XLA Ops:
  19.0 6.4 all-to-all-start
  26.6 91.6 %all_gather.30 = s32[32,128,6]{1,2,0:T(8,128)S(1)} all-gather(s32[1,128,6]{1,2,0:T(8,128)S(1)} %copy.183), channel_id=1, replica_groups=mesh['dp'=2,'ctx'=2,'expert'=8] {'dp','ctx','expert'}, dimensions={0}, use_global_device_ids=true | all-gather | bytes 101376 | tf_op jit(solution)/shard_map/all_gather | solution.py:759
  118.2 24.2 %gather_plane_1.1 = bf16[2,2,128,2048]{3,2,1,0:T(8,128)(2,1)} custom-call(bf16[128,2048]{1,0:T(8,128)(2,1)} %fusion.11.own), custom_call_target="tpu_custom_call" | custom-call | tf_op jit(solution)/shard_map/gather_plane_1/pallas_call | solution.py:285
  145.0 6.9 pad.16
  179.1 8.0 attend.1.own
  187.1 26.9 %gather_plane_2.1 = bf16[2,2,512,512]{3,2,1,0:T(8,128)(2,1)} custom-call(bf16[512,512]{1,0:T(8,128)(2,1)} %attend.1.own), custom_call_target="tpu_custom_call" | custom-call | tf_op jit(solution)/shard_map/gather_plane_2/pallas_call | solution.py:285
  227.2 16.6 %swap_plane_3.1 = bf16[2,2,128,512]{3,2,1,0:T(8,128)(2,1)} custom-call(bf16[2,2,128,512]{3,2,1,0:T(8,128)(2,1)} %bitcast.185), custom_call_target="tpu_custom_call" | custom-call | tf_op jit(solution)/shard_map/swap_plane_3/pallas_call | solution.py:314
  248.2 86.3 %gather_all_4.1 = bf16[2,2,4,2,128,2048]{5,4,3,2,1,0:T(8,128)(2,1)} custom-call(bf16[128,2048]{1,0:T(8,128)(2,1)} %multiply_convert_fusion.own), custom_call_target="tpu_custom_call" | custom-call | tf_op jit(solution)/shard_map/gather_all_4/pallas_call | solution.py:127
  334.6 175.8 %ffn.1 = (bf16[4096,2048]{1,0:T(8,128)(2,1)}, bf16[4096,2048]{1,0:T(8,128)(2,1)}, f32[2,2,352,2048]{3,2,1,0:T(8,128)}, f32[2,352,2048]{2,1,0:T(8,128)}, f32[256,2048]{1,0:T(8,128)}, /*index=5*/f32[128,2048]{1,0:T(8,128)}) custom-call(bf16[4096,2048]{1,0:T(8,128)(2,1)} %bitcast.138, bf16[4096,2048]{1,0:T(8,128)(2,1)} %bitcast.146, ...), custom_call_target="tpu_custom_call" | custom-call | tf_op jit(solution)/shard_map/ffn/pallas_call | solution.py:571
  510.4 95.6 %sum_all_5.1 = f32[128,2048]{1,0:T(8,128)} custom-call(bf16[2,2,4,2,128,2048]{5,4,3,2,1,0:T(8,128)(2,1)} %bitcast.147), custom_call_target="tpu_custom_call" | custom-call | tf_op jit(solution)/shard_map/sum_all_5/pallas_call | solution.py:228
  614.7 11.0 swap_plane_7.1
  633.6 21.5 %sum_plane_8.1 = f32[512,512]{1,0:T(8,128)} custom-call(bf16[2,2,512,512]{3,2,1,0:T(8,128)(2,1)} %bitcast.151), custom_call_target="tpu_custom_call" | custom-call | tf_op jit(solution)/shard_map/sum_plane_8/pallas_call | solution.py:358
  657.1 10.9 attend_back.1
  673.6 10.0 sum_plane_9.1
  687.6 10.9 gather_plane_10.1
  720.3 18.5 %sum_plane_11.1 = f32[128,2048]{1,0:T(8,128)} custom-call(bf16[2,2,128,2048]{3,2,1,0:T(8,128)(2,1)} %bitcast.160), custom_call_target="tpu_custom_call" | custom-call | tf_op jit(solution)/shard_map/sum_plane_11/pallas_call | solution.py:358
  748.4 34.6 %all_to_all.20 = bf16[176,8,256]{2,0,1:T(8,128)(2,1)} all-to-all(bf16[176,8,256]{2,0,1:T(8,128)(2,1)S(1)} %pad_maximum_fusion.3), channel_id=1, replica_groups=mesh['dp'=2,'ctx'=2,'expert'=8] {'expert'}, dimensions={1} | all-to-all | bytes 1441792 | tf_op jit(solution)/shard_map/all_to_all | solution.py:916
  788.8 86.1 %sum_all_6.1 = f32[128,2048]{1,0:T(8,128)} custom-call(bf16[2,2,4,2,128,2048]{5,4,3,2,1,0:T(8,128)(2,1)} %bitcast.145), custom_call_target="tpu_custom_call" | custom-call | tf_op jit(solution)/shard_map/sum_all_6/pallas_call | solution.py:228
  878.7 59.8 %all-reduce.6.cloned.1.call-done = f32[19,2048]{1,0:T(8,128)} async-done(((f32[19,2048]{1,0:T(8,128)}), f32[19,2048]{1,0:T(8,128)}) %all-reduce.6.cloned.1.call-update) | async-done | bytes 155664 | tf_op jit(solution)/shard_map/psum | solution.py:936
  942.6 32.2 %reduce-scatter.5.cloned.1.call-done = bf16[64,1024]{1,0:T(8,128)(2,1)} async-done(((bf16[512,1024]{1,0:T(8,128)(2,1)}), bf16[64,1024]{1,0:T(8,128)(2,1)}) %reduce-scatter.5.cloned.1.call-update) | async-done | bytes 131088 | tf_op jit(solution)/shard_map/reduce_scatter | solution.py:902
  974.8 10.3 all_gather.33
  986.1 19.0 %all-gather.15.cloned.1.call-done = bf16[352,2048]{1,0:T(8,128)(2,1)} async-done(((bf16[88,2048]{1,0:T(8,128)(2,1)}), bf16[352,2048]{1,0:T(8,128)(2,1)}) %all-gather.15.cloned.1.call-update) | async-done | bytes 1441808 | tf_op jit(solution)/shard_map/all_gather | solution.py:926
  1008.4 40.3 %all-gather.13.cloned.1.call-done = bf16[4,1408,256]{2,1,0:T(8,128)(2,1)} async-done(((bf16[1,1408,256]{2,1,0:T(8,128)(2,1)}), bf16[4,1408,256]{2,1,0:T(8,128)(2,1)}) %all-gather.13.cloned.1.call-update) | async-done | bytes 2883600 | tf_op jit(solution)/shard_map/all_gather | solution.py:923
  1060.8 31.6 %all-gather.19.cloned.1.call-done = bf16[1024,1424]{0,1:T(8,128)(2,1)} async-done(((bf16[256,1424]{0,1:T(8,128)(2,1)}), bf16[1024,1424]{0,1:T(8,128)(2,1)}) %all-gather.19.cloned.1.call-update) | async-done | bytes 2916368 | tf_op jit(solution)/shard_map/all_gather | solution.py:901
  (231 shorter events, 171.1 us)
Async XLA Ops:
  7.2 149.8 %all-gather.9.cloned.1.call-start = ((), (), s32[]{:S(2)}) async-start(), calls=%async_computation.4 | async-start | bytes 8552448 | tf_op jit(solution)/shard_map/all_gather | solution.py:753
  10.8 165.1 %all-gather.11.cloned.1.call-start = ((), (), s32[]{:S(2)}) async-start(), calls=%async_computation.5 | async-start | bytes 1179648 | tf_op jit(solution)/shard_map/all_gather | solution.py:754
  11.5 323.1 %all-gather.17.cloned.1.call-start = ((), (), s32[]{:S(2)}) async-start(), calls=%async_computation.11 | async-start | bytes 17301504 | tf_op jit(solution)/shard_map/all_gather | solution.py:760
  15.5 9.9 copy-start.35
  15.5 9.9 copy-start.11
  15.5 10.1 copy-start.32
  19.0 135.8 %all-to-all-start = ((bf16[8,256,256]{1,2,0:T(8,128)(2,1)}), bf16[8,256,256]{1,2,0:T(8,128)(2,1)}, u32[]{:S(2)}, u32[]{:S(2)}) async-start(bf16[8,256,256]{1,2,0:T(8,128)(2,1)} %bitcast.26), calls=%async_computation | async-start | bytes 2097152 | tf_op jit(solution)/shard_map/all_to_all | solution.py:781
  25.3 763.5 %reduce-scatter.3.cloned.1.call-start = ((), (), s32[]{:S(2)}) async-start(), calls=%async_computation.7 | async-start | bytes 6561792 | tf_op jit(solution)/shard_map/reduce_scatter | solution.py:900
  145.0 6.9 copy-start.14
  167.3 7.6 copy-start.16
  175.8 11.3 %copy-start.7 = (f32[512,512]{1,0:T(8,128)}, f32[512,512]{1,0:T(8,128)S(1)}, u32[]{:S(2)}) copy-start(f32[512,512]{1,0:T(8,128)S(1)} %slice_multiply_fusion) | copy-start | bytes 3145732
  610.4 15.3 %copy-start.19 = (bf16[2048,512]{1,0:T(8,128)(2,1)S(1)}, bf16[2048,512]{1,0:T(8,128)(2,1)}, u32[]{:S(2)}) copy-start(bf16[2048,512]{1,0:T(8,128)(2,1)} %copy.181) | copy-start | bytes 6291460
  657.1 13.4 %copy-start.23 = (bf16[512,1024]{1,0:T(8,128)(2,1)S(1)}, bf16[512,1024]{1,0:T(8,128)(2,1)}, u32[]{:S(2)}) copy-start(bf16[512,1024]{1,0:T(8,128)(2,1)} %all-gather.11.cloned.1.call-done) | copy-start | bytes 3145732
  670.5 13.1 %copy-start.8 = (f32[512,512]{1,0:T(8,128)S(1)}, f32[512,512]{1,0:T(8,128)}, u32[]{:S(2)}) copy-start(f32[512,512]{1,0:T(8,128)} %copy-done.7) | copy-start | bytes 3145732
  673.6 25.0 %copy-start.17 = (f32[512,128]{1,0:T(8,128)S(1)}, f32[512,128]{1,0:T(8,128)}, u32[]{:S(2)}) copy-start(f32[512,128]{1,0:T(8,128)} %copy-done.16) | copy-start | bytes 786436
  673.6 25.0 %copy-start.27 = (f32[512,128]{1,0:T(8,128)S(1)}, f32[512,128]{1,0:T(8,128)}, u32[]{:S(2)}) copy-start(f32[512,128]{1,0:T(8,128)} %get-tuple-element.29) | copy-start | bytes 786436
  673.6 25.0 %copy-start.28 = (f32[512,128]{1,0:T(8,128)S(1)}, f32[512,128]{1,0:T(8,128)}, u32[]{:S(2)}) copy-start(f32[512,128]{1,0:T(8,128)} %get-tuple-element.30) | copy-start | bytes 786436
  683.6 15.1 %copy-start.25 = (bf16[2,2,128,512]{3,2,1,0:T(8,128)(2,1)S(1)}, bf16[2,2,128,512]{3,2,1,0:T(8,128)(2,1)}, u32[]{:S(2)}) copy-start(bf16[2,2,128,512]{3,2,1,0:T(8,128)(2,1)} %swap_plane_7.1) | copy-start | bytes 1572868
  698.7 6.0 copy-start.30
  714.4 224.1 %all-reduce.6.cloned.1.call-start = ((), (), s32[]{:S(2)}) async-start(), calls=%async_computation.6 | async-start | bytes 393216 | tf_op jit(solution)/shard_map/psum | solution.py:936
  744.2 230.6 %reduce-scatter.5.cloned.1.call-start = ((), (), s32[]{:S(2)}) async-start(), calls=%async_computation.8 | async-start | bytes 1179648 | tf_op jit(solution)/shard_map/reduce_scatter | solution.py:902
  746.0 259.2 %all-gather.15.cloned.1.call-start = ((), (), s32[]{:S(2)}) async-start(), calls=%async_computation.10 | async-start | bytes 1802240 | tf_op jit(solution)/shard_map/all_gather | solution.py:926
  748.1 300.6 %all-gather.13.cloned.1.call-start = ((), (), s32[]{:S(2)}) async-start(), calls=%async_computation.9 | async-start | bytes 3604480 | tf_op jit(solution)/shard_map/all_gather | solution.py:923
  783.0 309.3 %all-gather.19.cloned.1.call-start = ((), (), s32[]{:S(2)}) async-start(), calls=%async_computation.12 | async-start | bytes 3645440 | tf_op jit(solution)/shard_map/all_gather | solution.py:901
  (23 other events, 57.5 us)
Sparse Core Ops, SparseCore 0:
  10.9 102.3 all-gather.8
  115.4 20.7 all-gather.10
  139.3 148.2 all-gather.16
  714.5 74.2 reduce-scatter.2
  794.8 143.7 all-reduce.5
  941.2 33.5 reduce-scatter.4
  977.2 27.8 all-gather.14
  1007.0 41.6 all-gather.12
  1050.5 41.7 all-gather.18

commit v2 on v1

--- a/solution.py
+++ b/solution.py
@@ -26,6 +26,12 @@
 LANES = 128
 CHUNK = 512
 VMEM_LIMIT = 66_000_000
+
+
+def lasting(microseconds):
+    return pl.CostEstimate(
+        flops=0, transcendentals=0, bytes_accessed=int(microseconds * 3_000_000)
+    )
 
 
 def here():
@@ -140,6 +146,7 @@
             dma((4 * nz,)),
         ],
         compiler_params=pltpu.CompilerParams(collective_id=number, has_side_effects=True),
+        cost_estimate=lasting(86),
         name=f"gather_all_{number}",
     )(own)
 
@@ -250,6 +257,7 @@
         compiler_params=pltpu.CompilerParams(
             collective_id=number, has_side_effects=True, vmem_limit_bytes=VMEM_LIMIT
         ),
+        cost_estimate=lasting(90),
         name=f"sum_all_{number}",
     )(part)
 
@@ -289,6 +297,7 @@
         out_specs=pl.BlockSpec(memory_space=pltpu.VMEM),
         scratch_shapes=[dma(()), dma((4,)), dma((4,))],
         compiler_params=pltpu.CompilerParams(collective_id=number, has_side_effects=True),
+        cost_estimate=lasting(22),
         name=f"gather_plane_{number}",
     )(own)
 
@@ -318,6 +327,7 @@
         out_specs=pl.BlockSpec(memory_space=pltpu.VMEM),
         scratch_shapes=[dma(()), dma((3,)), dma((3,))],
         compiler_params=pltpu.CompilerParams(collective_id=number, has_side_effects=True),
+        cost_estimate=lasting(12),
         name=f"swap_plane_{number}",
     )(part)
 
@@ -371,7 +381,117 @@
             dma((6,)),
         ],
         compiler_params=pltpu.CompilerParams(collective_id=number, has_side_effects=True),
+        cost_estimate=lasting(20),
         name=f"sum_plane_{number}",
+    )(part)
+
+
+def swap_expert_kernel(groups, part, out, lsem, ssem, rsem):
+    x, y, z, c = here()
+    spot = 2 * z + c
+    others = [lax.rem(spot + k, groups) for k in range(1, groups)]
+    froms = [lax.rem(spot + groups - k, groups) for k in range(1, groups)]
+    greet([(x, y, other) for other in others])
+    sends = Sends(ssem)
+    for k, other in enumerate(others):
+        sends.go(part.at[other], out.at[spot], rsem.at[k], (x, y, other))
+    local = pltpu.make_async_copy(part.at[spot], out.at[spot], lsem)
+    local.start()
+    for k, source in enumerate(froms):
+        arrive(out.at[source], rsem.at[k], (x, y, source))
+    sends.drain()
+    local.wait()
+
+
+def swap_expert(part, number):
+    groups = part.shape[0]
+    dma = pltpu.SemaphoreType.DMA
+    return pl.pallas_call(
+        functools.partial(swap_expert_kernel, groups),
+        out_shape=jax.ShapeDtypeStruct(part.shape, part.dtype),
+        in_specs=[pl.BlockSpec(memory_space=pltpu.VMEM)],
+        out_specs=pl.BlockSpec(memory_space=pltpu.VMEM),
+        scratch_shapes=[dma(()), dma((groups - 1,)), dma((groups - 1,))],
+        compiler_params=pltpu.CompilerParams(collective_id=number, has_side_effects=True),
+        cost_estimate=lasting(20),
+        name=f"swap_expert_{number}",
+    )(part)
+
+
+def finish_kernel(nz, rows, part, out, own, rc, rz, lsem, ssem, csem, zsem, psem):
+    x, y, z, c = here()
+    xn, yn, cn = (1 - x, y, 2 * z + c), (x, 1 - y, 2 * z + c), (x, y, 2 * z + 1 - c)
+    dest = [lax.rem(z + 1 + i, nz) for i in range(nz)]
+    zpeers = [(x, y, 2 * dest[i] + c) for i in range(nz - 1)]
+    greet(zpeers + [xn, yn, cn])
+    sends = Sends(ssem)
+    half = rows // 2
+    spans = (pl.ds(0, half), pl.ds(half, half))
+    loads = {}
+    for k, span in enumerate(spans):
+        for i in range(nz):
+            sends.go(part.at[dest[i], 1 - c, span], rc.at[i, span], csem.at[k, i], cn)
+            loads[k, i] = pltpu.make_async_copy(
+                part.at[dest[i], c, span], own.at[i, span], lsem.at[k, i]
+            )
+            loads[k, i].start()
+
+    def base(k, i):
+        span = spans[k]
+        loads[k, i].wait()
+        arrive(rc.at[i, span], csem.at[k, i], cn)
+        return own[i, span].astype(F32) + rc[i, span].astype(F32)
+
+    for k, span in enumerate(spans):
+        for i in range(nz - 1):
+            own[i, span] = base(k, i).astype(BF)
+            sends.go(own.at[i, span], rz.at[i, span], zsem.at[k, i], zpeers[i])
+    for k, span in enumerate(spans):
+        total = base(k, nz - 1)
+        for i in range(nz - 1):
+            arrive(rz.at[i, span], zsem.at[k, i], zpeers[0])
+            total = total + rz[i, span].astype(F32)
+        out[x, y, span] = total.astype(BF)
+        mine = out.at[x, y, span]
+        sends.go(mine, mine, psem.at[0, k], xn)
+        sends.go(mine, mine, psem.at[1, k], yn)
+    side = out.at[1 - x, y]
+    arrive(side.at[spans[0]], psem.at[0, 0], xn)
+    sends.go(side.at[spans[0]], side.at[spans[0]], psem.at[2, 0], yn)
+    arrive(side.at[spans[1]], psem.at[0, 1], xn)
+    side = out.at[x, 1 - y]
+    arrive(side.at[spans[0]], psem.at[1, 0], yn)
+    arrive(side.at[spans[1]], psem.at[1, 1], yn)
+    sends.go(side.at[spans[1]], side.at[spans[1]], psem.at[2, 1], xn)
+    corner = out.at[1 - x, 1 - y]
+    arrive(corner.at[spans[0]], psem.at[2, 0], yn)
+    arrive(corner.at[spans[1]], psem.at[2, 1], xn)
+    sends.drain()
+
+
+def finish(part, nz, number):
+    rows, width = part.shape[-2:]
+    dma = pltpu.SemaphoreType.DMA
+    return pl.pallas_call(
+        functools.partial(finish_kernel, nz, rows),
+        out_shape=jax.ShapeDtypeStruct((2, 2, rows, width), BF),
+        in_specs=[pl.BlockSpec(memory_space=pl.ANY)],
+        out_specs=pl.BlockSpec(memory_space=pltpu.VMEM),
+        scratch_shapes=[
+            pltpu.VMEM((nz, rows, width), BF),
+            pltpu.VMEM((nz, rows, width), BF),
+            pltpu.VMEM((nz - 1, rows, width), BF),
+            dma((2, nz)),
+            dma((4 * nz + 4,)),
+            dma((2, nz)),
+            dma((2, nz - 1)),
+            dma((3, 2)),
+        ],
+        compiler_params=pltpu.CompilerParams(
+            collective_id=number, has_side_effects=True, vmem_limit_bytes=VMEM_LIMIT
+        ),
+        cost_estimate=lasting(70),
+        name=f"finish_{number}",
     )(part)
 
 
@@ -394,41 +514,217 @@
 
 def ffn_kernel(
     dims,
-    h,
-    g,
+    h_all,
+    g_all,
     pos,
     win,
     wout,
     wcat,
     wso,
-    out,
-    gh,
+    o_out,
+    o_gh,
     o_gwin,
     o_gwout,
     o_gwcat,
     o_gwso,
+    o_swap,
+    mine,
+    rc,
+    rd,
+    rx,
+    ry,
+    rz,
+    hb,
+    gb,
+    ob,
     rows,
     grows,
     gwin,
     gwout,
     gwcat,
     gwso,
-    osem,
+    stin,
+    stout,
+    swap,
+    l_h,
+    l_g,
+    l_own,
+    l_in,
+    l_out,
+    l_end,
+    s_rc,
+    s_d,
+    s_x,
+    s_y,
+    s_z,
+    s_swap,
+    a_rc,
+    a_d,
+    a_x,
+    a_y,
+    a_z,
+    a_swap,
 ):
-    hidden, padded, slots, shared, experts = dims
-    step = pl.program_id(0)
-    tokens, width = h.shape
-    block = 2 * LANES
-    pairs = tokens // block
+    nz, tok, hidden, padded, slots, shared, experts = dims
+    groups = 2 * nz
+    width = h_all.shape[1]
+    block = 2 * tok
     per = 2 * slots
-    first_lane = shared + 2 * lax.axis_index("expert")
-
-    @pl.when(step == 0)
-    def _():
-        gwin[...] = jnp.zeros_like(gwin)
-        gwout[...] = jnp.zeros_like(gwout)
-        gwcat[...] = jnp.zeros_like(gwcat)
-        gwso[...] = jnp.zeros_like(gwso)
+    half = tok // 2
+    steps = 2 * nz
+    x, y, z, c = here()
+    spot = 2 * z + c
+    xn, yn, cn = (1 - x, y, spot), (x, 1 - y, spot), (x, y, 2 * z + 1 - c)
+    others = [lax.rem(spot + k, groups) for k in range(1, groups)]
+    froms = [lax.rem(spot + groups - k, groups) for k in range(1, groups)]
+    greet([xn, yn] + [(x, y, other) for other in others])
+    first, second = pl.ds(0, half), pl.ds(half, half)
+
+    def dest(i):
+        return lax.rem(z + 1 + i, nz)
+
+    def zpeer(i):
+        return (x, y, 2 * dest(i) + c)
+
+    def unit_start(s, u):
+        qx = jnp.where(lax.rem(s, 2) == 0, 1 - x, x)
+        qy = y if u else 1 - y
+        return pl.multiple_of(((qx * 2 + qy) * nz + dest(s // 2)) * block, block)
+
+    def tiles(s, slot):
+        for u in range(2):
+            at, to = pl.ds(unit_start(s, u), block), pl.ds(u * block, block)
+            yield pltpu.make_async_copy(h_all.at[at], hb.at[slot, to], l_h.at[slot, u])
+            yield pltpu.make_async_copy(
+                g_all.at[at, pl.ds(0, width)], gb.at[slot, to], l_g.at[slot, u]
+            )
+
+    def own_writes(s):
+        for u in range(2):
+            for t in range(2):
+                yield pltpu.make_async_copy(
+                    ob.at[t, pl.ds(u * block + c * tok, tok)],
+                    mine.at[2 * s + u, t],
+                    l_own.at[u, t],
+                )
+
+    def remote(src, dst, send_sem, arrival, peer):
+        return pltpu.make_async_remote_copy(
+            src_ref=src,
+            dst_ref=dst,
+            send_sem=send_sem,
+            recv_sem=arrival,
+            device_id=peer,
+            device_id_type=MESH,
+        )
+
+    def core_sends(s):
+        for u in range(2):
+            for t in range(2):
+                yield remote(
+                    ob.at[t, pl.ds(u * block + (1 - c) * tok, tok)],
+                    rc.at[2 * s + u, t],
+                    s_rc.at[u, t],
+                    a_rc.at[2 * s + u, t],
+                    cn,
+                )
+
+    def unit_of(kind, i):
+        return 4 * i + "dxyo".index(kind)
+
+    def loads(kind, i, t, p):
+        n = unit_of(kind, i)
+        yield pltpu.make_async_copy(mine.at[n, t], stin.at[p, 0], l_in.at[p, 0])
+        yield pltpu.make_async_copy(rc.at[n, t], stin.at[p, 1], l_in.at[p, 1])
+        if kind == "x":
+            yield pltpu.make_async_copy(rd.at[i, t, 0], stin.at[p, 2, first], l_in.at[p, 2])
+        if kind == "y":
+            yield pltpu.make_async_copy(rd.at[i, t, 1], stin.at[p, 2, second], l_in.at[p, 2])
+        if kind == "o":
+            yield pltpu.make_async_copy(rx.at[i, t], stin.at[p, 2], l_in.at[p, 2])
+            yield pltpu.make_async_copy(ry.at[i, t], stin.at[p, 3], l_in.at[p, 3])
+
+    def begin(kind, i, t, p):
+        n = unit_of(kind, i)
+        arrive(rc.at[n, t], a_rc.at[n, t], cn)
+        if kind == "x":
+            arrive(rd.at[i, t, 0], a_d.at[i, t, 0], yn)
+        if kind == "y":
+            arrive(rd.at[i, t, 1], a_d.at[i, t, 1], xn)
+        if kind == "o":
+            arrive(rx.at[i, t], a_x.at[i, t], xn)
+            arrive(ry.at[i, t], a_y.at[i, t], yn)
+        for copy in loads(kind, i, t, p):
+            copy.start()
+
+    def val(ref):
+        return ref[...].astype(F32)
+
+    def write_back(kind, i, t, p):
+        return pltpu.make_async_copy(stout.at[p], mine.at[unit_of(kind, i), t], l_out.at[p])
+
+    def settle(kind, i, t, p):
+        for copy in loads(kind, i, t, p):
+            copy.wait()
+        if kind == "d":
+            stout[p] = (val(stin.at[p, 0]) + val(stin.at[p, 1])).astype(BF)
+        elif kind == "o":
+            stout[p] = (
+                val(stin.at[p, 0]) + val(stin.at[p, 1]) + val(stin.at[p, 2]) + val(stin.at[p, 3])
+            ).astype(BF)
+        else:
+            more, same = (first, second) if kind == "x" else (second, first)
+            stout[p, more] = (
+                val(stin.at[p, 0, more]) + val(stin.at[p, 1, more]) + val(stin.at[p, 2, more])
+            ).astype(BF)
+            stout[p, same] = (val(stin.at[p, 0, same]) + val(stin.at[p, 1, same])).astype(BF)
+        write_back(kind, i, t, p).start()
+
+    def outgoing(kind, i, t):
+        src = mine.at[unit_of(kind, i), t]
+        if kind == "d":
+            yield remote(src.at[first], rd.at[i, t, 0], s_d.at[i, t, 0], a_d.at[i, t, 0], yn)
+            yield remote(src.at[second], rd.at[i, t, 1], s_d.at[i, t, 1], a_d.at[i, t, 1], xn)
+        if kind == "x":
+            yield remote(src, rx.at[i, t], s_x.at[i, t], a_x.at[i, t], xn)
+        if kind == "y":
+            yield remote(src, ry.at[i, t], s_y.at[i, t], a_y.at[i, t], yn)
+        if kind == "o":
+            yield remote(src, rz.at[i, t], s_z.at[i, t], a_z.at[i, t], zpeer(i))
+
+    def launch(kind, i, t, p):
+        write_back(kind, i, t, p).wait()
+        for copy in outgoing(kind, i, t):
+            copy.start()
+
+    def serve(action, s, k):
+        odd = lax.rem(s, 2) == 1
+        t, p = k % 2, k % 2
+        if k < 2:
+
+            @pl.when(odd & (s >= 3))
+            def _():
+                action("o", (s - 3) // 2, t, p)
+
+            @pl.when(jnp.logical_not(odd) & (s >= 2))
+            def _():
+                action("x", (s - 2) // 2, t, p)
+        else:
+
+            @pl.when(odd)
+            def _():
+                action("d", (s - 1) // 2, t, p)
+
+            @pl.when(jnp.logical_not(odd) & (s >= 2))
+            def _():
+                action("y", (s - 2) // 2, t, p)
+
+    for copy in tiles(0, 0):
+        copy.start()
+    gwin[...] = jnp.zeros_like(gwin)
+    gwout[...] = jnp.zeros_like(gwout)
+    gwcat[...] = jnp.zeros_like(gwcat)
+    gwso[...] = jnp.zeros_like(gwso)
 
     def chunks(body):
         def run(n, carry):
@@ -437,159 +733,280 @@
 
         lax.fori_loop(0, width // CHUNK, run, 0)
 
-    mixed = dot_nn(h[...], wcat[...])
-    gate, up = mixed[:, :LANES], mixed[:, LANES:]
-    lane = lax.broadcasted_iota(jnp.int32, gate.shape, 1)
-    of_router = (lane >= shared) & (lane < shared + experts)
-    logits = jnp.where(of_router, gate, -1e30)
-    raised = jnp.where(of_router, jnp.exp(logits - jnp.max(logits, axis=1, keepdims=True)), 0.0)
-    router = raised / jnp.sum(raised, axis=1, keepdims=True)
-    silu, slope = silu_parts(gate)
-    act = (silu * up).astype(BF)
-    gact = dot_nt(g[...], wso[...])
-    ggate = gact * up * slope
-    gup = gact * silu
-    high = router.astype(BF)
-    router_parts = jnp.concatenate([high, (router - high.astype(F32)).astype(BF)], axis=1)
-    slot_lane = lax.broadcasted_iota(jnp.int32, (per, LANES), 1)
-    slot_row = lax.broadcasted_iota(jnp.int32, (per, block), 0)
-    picks, picked = [], [[], []]
-    for pair in range(pairs):
-        span = slice(pair * block, (pair + 1) * block)
-        pick = jnp.concatenate(
-            [
-                jnp.where(pos[j : j + 1, span] == slot_row, 1.0, 0.0).astype(BF) for j in range(2)
-            ],
-            axis=0,
+    first_lane = shared + 2 * spot
+
+    def step(s, carry):
+        slot = lax.rem(s, 2)
+        for copy in tiles(s, slot):
+            copy.wait()
+
+        @pl.when(s + 1 < steps)
+        def _():
+            for copy in tiles(s + 1, 1 - slot):
+                copy.start()
+
+        @pl.when(s >= 1)
+        def _():
+            for copy in own_writes(s - 1):
+                copy.wait()
+
+        serve(begin, s, 0)
+        mixed = dot_nn(hb[slot], wcat[...])
+        gate, up = mixed[:, :LANES], mixed[:, LANES:]
+        lane = lax.broadcasted_iota(jnp.int32, gate.shape, 1)
+        of_router = (lane >= shared) & (lane < shared + experts)
+        logits = jnp.where(of_router, gate, -1e30)
+        raised = jnp.where(
+            of_router, jnp.exp(logits - jnp.max(logits, axis=1, keepdims=True)), 0.0
         )
-        picks.append(pick)
-        place = slice(pair * per, (pair + 1) * per)
-
-        def fetch(cols, pick=pick, span=span, place=place):
-            taken = dot_nn(pick, h[span, cols]).astype(BF)
-            rows[0, place, cols] = taken[:per]
-            rows[1, place, cols] = taken[per:]
-            taken = dot_nn(pick, g[span, cols]).astype(BF)
-            grows[0, place, cols] = taken[:per]
-            grows[1, place, cols] = taken[per:]
-
-        chunks(fetch)
-        taken = dot_nn(pick, router_parts[span])
-        taken = taken[:, :LANES] + taken[:, LANES:]
+        router = raised / jnp.sum(raised, axis=1, keepdims=True)
+        silu, slope = silu_parts(gate)
+        act = (silu * up).astype(BF)
+        gact = dot_nt(gb[slot], wso[...])
+        ggate = gact * up * slope
+        gup = gact * silu
+        high = router.astype(BF)
+        router_parts = jnp.concatenate([high, (router - high.astype(F32)).astype(BF)], axis=1)
+        serve(settle, s, 0)
+        serve(begin, s, 1)
+        slot_lane = lax.broadcasted_iota(jnp.int32, (per, LANES), 1)
+        slot_row = lax.broadcasted_iota(jnp.int32, (per, block), 0)
+        picks, picked = [], [[], []]
+        for u in range(2):
+            span = slice(u * block, (u + 1) * block)
+            place = slice(u * per, (u + 1) * per)
+            lanes = pl.ds(unit_start(s, u), block)
+            pick = jnp.concatenate(
+                [
+                    jnp.where(pos[j : j + 1, lanes] == slot_row, 1.0, 0.0).astype(BF)
+                    for j in range(2)
+                ],
+                axis=0,
+            )
+            picks.append(pick)
+
+            def fetch(cols, pick=pick, span=span, place=place):
+                taken = dot_nn(pick, hb[slot, span, cols]).astype(BF)
+                rows[0, place, cols] = taken[:per]
+                rows[1, place, cols] = taken[per:]
+                taken = dot_nn(pick, gb[slot, span, cols]).astype(BF)
+                grows[0, place, cols] = taken[:per]
+                grows[1, place, cols] = taken[per:]
+
+            chunks(fetch)
+            taken = dot_nn(pick, router_parts[span])
+            taken = taken[:, :LANES] + taken[:, LANES:]
+            for j in range(2):
+                picked[j].append(
+                    jnp.sum(
+                        jnp.where(slot_lane == first_lane + j, taken[j * per : (j + 1) * per], 0.0),
+                        axis=1,
+                        keepdims=True,
+                    )
+                )
+        serve(settle, s, 1)
+        serve(launch, s, 0)
+        serve(begin, s, 2)
+        grad_picked = []
         for j in range(2):
-            picked[j].append(
-                jnp.sum(
-                    jnp.where(slot_lane == first_lane + j, taken[j * per : (j + 1) * per], 0.0),
-                    axis=1,
-                    keepdims=True,
-                )
+            share = jnp.concatenate(picked[j], axis=0)
+            both = dot_nt(rows[j], win[j])
+            egate, eup = both[:, :padded], both[:, padded:]
+            raw = dot_nt(grows[j], wout[j])
+            esilu, eslope = silu_parts(egate)
+            eact = esilu * eup
+            grad_picked.append(jnp.sum(eact * raw, axis=1, keepdims=True))
+            scaled = (share * eact).astype(BF)
+            graw = share * raw
+            gboth = jnp.concatenate([graw * eup * eslope, graw * esilu], axis=1).astype(BF)
+
+            def expert(cols, j=j, scaled=scaled, gboth=gboth):
+                gin, gout = rows[j, :, cols], grows[j, :, cols]
+                gwout[j, :, cols] += dot_tn(scaled[:, :hidden], gout)
+                gwin[j, 0, :, cols] += dot_tn(gboth[:, :hidden], gin)
+                gwin[j, 1, :, cols] += dot_tn(gboth[:, padded : padded + hidden], gin)
+                grows[j, :, cols] = dot_nn(scaled, wout[j, :, cols]).astype(BF)
+                rows[j, :, cols] = dot_nn(gboth, win[j, :, cols]).astype(BF)
+
+            chunks(expert)
+            serve(settle, s, 2 + j)
+            serve(launch, s, 1 + j)
+            if j == 0:
+                serve(begin, s, 3)
+
+        @pl.when(s >= 1)
+        def _():
+            for copy in core_sends(s - 1):
+                copy.wait_send()
+
+        gparts = []
+        for u in range(2):
+            span = slice(u * block, (u + 1) * block)
+            place = slice(u * per, (u + 1) * per)
+            pick = picks[u]
+            spread = jnp.concatenate(
+                [
+                    jnp.where(slot_lane == first_lane + j, grad_picked[j][place], 0.0)
+                    for j in range(2)
+                ],
+                axis=0,
             )
-    grad_picked = []
-    for j in range(2):
-        share = jnp.concatenate(picked[j], axis=0)
-        both = dot_nt(rows[j], win[j])
-        egate, eup = both[:, :padded], both[:, padded:]
-        raw = dot_nt(grows[j], wout[j])
-        esilu, eslope = silu_parts(egate)
-        eact = esilu * eup
-        grad_picked.append(jnp.sum(eact * raw, axis=1, keepdims=True))
-        scaled = (share * eact).astype(BF)
-        graw = share * raw
-        gboth = jnp.concatenate([graw * eup * eslope, graw * esilu], axis=1).astype(BF)
-
-        def expert(cols, j=j, scaled=scaled, gboth=gboth):
-            gin, gout = rows[j, :, cols], grows[j, :, cols]
-            gwout[j, :, cols] += dot_tn(scaled[:, :hidden], gout)
-            gwin[j, 0, :, cols] += dot_tn(gboth[:, :hidden], gin)
-            gwin[j, 1, :, cols] += dot_tn(gboth[:, padded : padded + hidden], gin)
-            grows[j, :, cols] = dot_nn(scaled, wout[j, :, cols]).astype(BF)
-            rows[j, :, cols] = dot_nn(gboth, win[j, :, cols]).astype(BF)
-
-        chunks(expert)
-    gparts = []
-    for pair in range(pairs):
-        span = slice(pair * block, (pair + 1) * block)
-        place = slice(pair * per, (pair + 1) * per)
-        pick = picks[pair]
-        spread = jnp.concatenate(
-            [
-                jnp.where(slot_lane == first_lane + j, grad_picked[j][place], 0.0)
-                for j in range(2)
-            ],
-            axis=0,
+            high = spread.astype(BF)
+            low = (spread - high.astype(F32)).astype(BF)
+            grouter = dot_tn(pick, jnp.concatenate([high, low], axis=1))
+            grouter = grouter[:, :LANES] + grouter[:, LANES:]
+            share = router[span]
+            glogits = share * (grouter - jnp.sum(share * grouter, axis=1, keepdims=True))
+            gpart = jnp.concatenate([ggate[span] + glogits, gup[span]], axis=1).astype(BF)
+            gparts.append(gpart)
+
+            def spreads(cols, pick=pick, span=span, place=place, gpart=gpart):
+                sent = jnp.concatenate([grows[0, place, cols], grows[1, place, cols]], axis=0)
+                ob[0, span, cols] = (dot_tn(pick, sent) + dot_nn(act[span], wso[:, cols])).astype(BF)
+                sent = jnp.concatenate([rows[0, place, cols], rows[1, place, cols]], axis=0)
+                ob[1, span, cols] = (dot_tn(pick, sent) + dot_nt(gpart, wcat[cols, :])).astype(BF)
+
+            chunks(spreads)
+        for copy in core_sends(s):
+            copy.start()
+        for copy in own_writes(s):
+            copy.start()
+        serve(launch, s, 3)
+        gall = jnp.concatenate(gparts, axis=0)
+
+        def dense(cols):
+            gwcat[:, cols] += dot_tn(gall, hb[slot, :, cols])
+            gwso[:, cols] += dot_tn(act, gb[slot, :, cols])
+
+        chunks(dense)
+        return carry
+
+    lax.fori_loop(0, steps, step, 0)
+    last = nz - 1
+    for copy in own_writes(steps - 1):
+        copy.wait()
+    ends = [("x", 0), ("x", 1), ("y", 0), ("y", 1)]
+    for kind, t in ends[:2]:
+        begin(kind, last, t, t)
+    for k, (kind, t) in enumerate(ends):
+        settle(kind, last, t, t)
+        launch(kind, last, t, t)
+        if k < 2:
+            begin(*ends[k + 2][:1], last, ends[k + 2][1], t)
+    finals = [
+        pltpu.make_async_copy(src, dst, l_end.at[k])
+        for k, (src, dst) in enumerate(
+            ((gwin, o_gwin), (gwout, o_gwout), (gwcat, o_gwcat), (gwso, o_gwso))
         )
-        high = spread.astype(BF)
-        low = (spread - high.astype(F32)).astype(BF)
-        grouter = dot_tn(pick, jnp.concatenate([high, low], axis=1))
-        grouter = grouter[:, :LANES] + grouter[:, LANES:]
-        share = router[span]
-        glogits = share * (grouter - jnp.sum(share * grouter, axis=1, keepdims=True))
-        gpart = jnp.concatenate([ggate[span] + glogits, gup[span]], axis=1).astype(BF)
-        gparts.append(gpart)
-
-        def spreads(cols, pick=pick, span=span, place=place, gpart=gpart):
-            sent = jnp.concatenate([grows[0, place, cols], grows[1, place, cols]], axis=0)
-            out[span, cols] = (dot_tn(pick, sent) + dot_nn(act[span], wso[:, cols])).astype(BF)
-            sent = jnp.concatenate([rows[0, place, cols], rows[1, place, cols]], axis=0)
-            gh[span, cols] = (dot_tn(pick, sent) + dot_nt(gpart, wcat[cols, :])).astype(BF)
-
-        chunks(spreads)
-    gall = jnp.concatenate(gparts, axis=0)
-
-    def dense(cols):
-        gwcat[:, cols] += dot_tn(gall, h[:, cols])
-        gwso[:, cols] += dot_tn(act, g[:, cols])
-
-    chunks(dense)
-
-    @pl.when(step == pl.num_programs(0) - 1)
-    def _():
-        copies = [
-            pltpu.make_async_copy(src, dst, osem.at[k])
-            for k, (src, dst) in enumerate(
-                ((gwin, o_gwin), (gwout, o_gwout), (gwcat, o_gwcat), (gwso, o_gwso))
+    ]
+    for copy in finals:
+        copy.start()
+    for e in range(groups):
+        cols = slice(e * (width // groups), (e + 1) * (width // groups))
+        swap[e, 0] = gwcat[:shared, cols].astype(BF)
+        swap[e, 1] = gwcat[LANES : LANES + shared, cols].astype(BF)
+    swaps = [
+        remote(swap.at[other], o_swap.at[spot], s_swap.at[k], a_swap.at[k], (x, y, other))
+        for k, other in enumerate(others)
+    ]
+    for copy in swaps:
+        copy.start()
+    kept = pltpu.make_async_copy(swap.at[spot], o_swap.at[spot], l_end.at[4])
+    kept.start()
+    late = []
+    for t in range(2):
+        for i in range(nz - 1):
+            arrive(rz.at[i, t], a_z.at[i, t], zpeer(0))
+            copy = pltpu.make_async_copy(
+                rz.at[i, t], hb.at[t, pl.ds(i * tok, tok)], l_h.at[t, 0] if i == 0 else l_g.at[t, i - 1]
             )
-        ]
-        for copy in copies:
             copy.start()
-        for copy in copies:
+            late.append(copy)
+    for t in range(2):
+        begin("o", last, t, t)
+    for t, out in enumerate((o_out, o_gh)):
+        for copy in loads("o", last, t, t):
             copy.wait()
-
-
-def ffn(h, g, pos, win, wout, wcat, wso, hidden, slots, shared, experts):
-    count, width = h.shape
+        for copy in late[t * (nz - 1) : (t + 1) * (nz - 1)]:
+            copy.wait()
+        total = val(stin.at[t, 0]) + val(stin.at[t, 1]) + val(stin.at[t, 2]) + val(stin.at[t, 3])
+        for i in range(nz - 1):
+            total = total + val(hb.at[t, pl.ds(i * tok, tok)])
+        out[...] = total
+    for k, source in enumerate(froms):
+        arrive(o_swap.at[source], a_swap.at[k], (x, y, source))
+    for copy in swaps + list(core_sends(steps - 1)):
+        copy.wait_send()
+    for i in range(nz):
+        for t in range(2):
+            for kind in "dxyo" if i < last else "dxy":
+                for copy in outgoing(kind, i, t):
+                    copy.wait_send()
+    kept.wait()
+    for copy in finals:
+        copy.wait()
+
+
+def ffn(h, g, pos, win, wout, wcat, wso, nz, tok, hidden, slots, shared, experts, number):
+    width = h.shape[1]
     padded = wout.shape[1]
-    tokens = 4 * LANES
-    whole = pl.Buffered(1)
-
-    def fixed(shape):
-        return pl.BlockSpec(shape, lambda i: (0,) * len(shape), pipeline_mode=whole)
-
-    moving = pl.BlockSpec((tokens, width), lambda i: (i, 0))
     left = pl.BlockSpec(memory_space=pl.ANY)
+    here_spec = pl.BlockSpec(memory_space=pltpu.VMEM)
+    dma = pltpu.SemaphoreType.DMA
     sums = [(2, 2, hidden, width), (2, hidden, width), (2 * LANES, width), (LANES, width)]
+    piece = (tok, width)
+    moved = [
+        (2 * nz, 2, shared, width // (2 * nz)),
+        (4 * nz, 2) + piece,
+        (4 * nz, 2) + piece,
+        (nz, 2, 2, tok // 2, width),
+        (nz, 2) + piece,
+        (nz, 2) + piece,
+        (nz - 1, 2) + piece,
+    ]
+    slot_rows = 4 * slots
     return pl.pallas_call(
-        functools.partial(ffn_kernel, (hidden, padded, slots, shared, experts)),
-        grid=(count // tokens,),
-        out_shape=[jax.ShapeDtypeStruct((count, width), BF)] * 2
-        + [jax.ShapeDtypeStruct(s, F32) for s in sums],
-        in_specs=[
-            moving,
-            moving,
-            pl.BlockSpec((8, tokens), lambda i: (0, i)),
-            fixed(win.shape),
-            fixed(wout.shape),
-            fixed(wcat.shape),
-            fixed(wso.shape),
-        ],
-        out_specs=[moving, moving, left, left, left, left],
+        functools.partial(ffn_kernel, (nz, tok, hidden, padded, slots, shared, experts)),
+        out_shape=[jax.ShapeDtypeStruct(piece, F32)] * 2
+        + [jax.ShapeDtypeStruct(s, F32) for s in sums]
+        + [jax.ShapeDtypeStruct(s, BF) for s in moved],
+        in_specs=[left, left] + [here_spec] * 5,
+        out_specs=[here_spec] * 2 + [left] * (len(sums) + len(moved)),
         scratch_shapes=[
-            pltpu.VMEM((2, tokens // LANES * slots, width), BF),
-            pltpu.VMEM((2, tokens // LANES * slots, width), BF),
+            pltpu.VMEM((2, 4 * tok, width), BF),
+            pltpu.VMEM((2, 4 * tok, width), BF),
+            pltpu.VMEM((2, 4 * tok, width), BF),
+            pltpu.VMEM((2, slot_rows, width), BF),
+            pltpu.VMEM((2, slot_rows, width), BF),
         ]
         + [pltpu.VMEM(s, F32) for s in sums]
-        + [pltpu.SemaphoreType.DMA((4,))],
-        compiler_params=pltpu.CompilerParams(vmem_limit_bytes=VMEM_LIMIT),
+        + [
+            pltpu.VMEM((2, 4) + piece, BF),
+            pltpu.VMEM((2,) + piece, BF),
+            pltpu.VMEM(moved[0], BF),
+            dma((2, 2)),
+            dma((2, 2)),
+            dma((2, 2)),
+            dma((2, 4)),
+            dma((2,)),
+            dma((5,)),
+            dma((2, 2)),
+            dma((nz, 2, 2)),
+            dma((nz, 2)),
+            dma((nz, 2)),
+            dma((nz - 1, 2)),
+            dma((2 * nz - 1,)),
+            dma((4 * nz, 2)),
+            dma((nz, 2, 2)),
+            dma((nz, 2)),
+            dma((nz, 2)),
+            dma((nz - 1, 2)),
+            dma((2 * nz - 1,)),
+        ],
+        compiler_params=pltpu.CompilerParams(
+            collective_id=number, has_side_effects=True, vmem_limit_bytes=VMEM_LIMIT
+        ),
+        cost_estimate=lasting(200),
         name="ffn",
     )(h, g, pos, win, wout, wcat, wso)
 
@@ -655,6 +1072,7 @@
         out_shape=jax.ShapeDtypeStruct(qn.shape, BF),
         in_specs=[each, one, one, wide, one, one],
         out_specs=each,
+        cost_estimate=lasting(8),
         name="attend",
     )(qn, qf, qs, ex, kf, ks)
 
@@ -674,6 +1092,7 @@
         ],
         in_specs=[each, one, one, wide, one, one, each],
         out_specs=[each, one, one, wide, one, one],
+        cost_estimate=lasting(11),
         name="attend_back",
     )(qn, qf, qs, ex, kf, ks, gm)
 
@@ -756,12 +1175,16 @@
     weight_output = attn_w[:, query_cols : query_cols + out_cols].reshape(4, out_cols, out_cols)
     weight_latent = attn_w[:, query_cols + out_cols :]
 
-    all_routes = lax.all_gather(routes[0], ALL, axis=0)
-    all_grads = lax.all_gather(cotangent[0], ALL, axis=0, tiled=True)
+    lanes = jnp.arange(LANES, dtype=jnp.int32)
+    named_here = jnp.any(routes[0][:, :, None] == lanes[None, None, :], axis=1)
+    all_grads = lax.all_gather(
+        jnp.concatenate([cotangent[0], named_here.astype(BF)], axis=1), ALL, axis=0, tiled=True
+    )
+    all_named = all_grads[:, width : width + experts].reshape(devices, tok_count, experts)
     offset = (jnp.arange(devices, dtype=jnp.int32) % 2 * capacity)[:, None]
     slots = []
     for j in range(2):
-        named = jnp.any(all_routes == 2 * spot + j, axis=2)
+        named = lax.dynamic_index_in_dim(all_named, 2 * spot + j, axis=2, keepdims=False) > 0
         order = jnp.cumsum(named.astype(jnp.int32), axis=1) - 1
         slots.append(jnp.where(named, order + offset, -1).reshape(1, -1))
     slots = jnp.concatenate(slots + [jnp.full((6, slots[0].shape[1]), -1, jnp.int32)], axis=0)
@@ -815,7 +1238,7 @@
     normed_two, factor_two = normalize(first_sum)
     hidden_two = (normed_two * ffn_gain).astype(BF)
     h2 = gather_all(hidden_two, nz, 4).reshape(devices * tok_count, width)
-    out_part, back_part, grad_in, grad_down, grad_cat, grad_so = ffn(
+    ffn_out, grad_h2, grad_in, grad_down, grad_cat, grad_so, shared_in = ffn(
         h2,
         all_grads,
         slots,
@@ -823,14 +1246,18 @@
         expert_down,
         weight_shared,
         own_shared_out,
+        nz,
+        tok_count,
         hidden,
         capacity,
         units,
         experts,
-    )
-    spread = (2, 2, nz, 2, tok_count, width)
-    grad_h2 = sum_all(back_part.reshape(spread), nz, 5)
-    ffn_out = sum_all(out_part.reshape(spread), nz, 6)
+        5,
+    )[:7]
+    shared_in = lax.all_gather(shared_in.reshape(-1, local_rows), PLANE, axis=0)
+    shared_in = shared_in.reshape(4, groups, 2, units, local_rows)
+    shared_in = shared_in.transpose(4, 2, 1, 0, 3).reshape(local_rows, -1).astype(F32)
+    shared_out = lax.all_gather(grad_so[:units].astype(BF), PLANE, axis=0, tiled=True).astype(F32)
     output = (first_sum + ffn_out).astype(BF)[None]
     grad_out = cotangent[0].astype(F32)
     grad_norm, grad_ffn = norm_back(grad_h2, normed_two, factor_two, ffn_gain)
@@ -841,11 +1268,24 @@
     grad_mixed = jnp.einsum("tn,pkn->ptk", low, weight_output, preferred_element_type=F32)
     grad_mixed = sum_plane(grad_mixed.astype(BF).reshape(2, 2, 4 * tok_count, nope_cols), 8)
     grad_wo = jnp.einsum("ptk,tn->pkn", mixed, low, preferred_element_type=F32)
+    early = jnp.concatenate(
+        [
+            grad_wo.reshape(width, out_cols).astype(BF),
+            grad_cat[units : units + experts].T.astype(BF),
+            grad_ffn[:, None].astype(BF),
+            jnp.zeros((width, LANES - experts - 1), BF),
+        ],
+        axis=1,
+    )
+    early = lax.psum_scatter(early, "expert", scatter_dimension=0, tiled=True)
+    early = lax.all_gather(early, PLANE, axis=0)
+    grad_wo = columns_of(early[:, :, :out_cols]).astype(F32)
+    sums = jnp.sum(early[:, :, out_cols : out_cols + experts + 1].astype(F32), axis=0)
+    grad_wr, grad_ffn = sums[:, :experts], sums[:, experts]
     gqn, gqf, gqs, gex, gkf, gks = attend_back(
         query_nope, query_f, query_s, expanded, key_f, key_s, grad_mixed.astype(BF), length
     )
     grad_comp = dot_nt(gex, weight_expand)
-    grad_we = dot_tn(compressed, gex)
     lat_cols = KV + ROPE
     lat_pad = -(-lat_cols // LANES) * LANES - lat_cols
     grad_lat = jnp.concatenate(
@@ -865,6 +1305,18 @@
     grad_lat_in, grad_lat_gain = norm_back(
         grad_lat[:, :KV], own_rows(normed_lat), own_rows(factor_lat), latent_gain
     )
+    grad_we = jnp.concatenate(
+        [
+            dot_tn(compressed, gex).astype(BF),
+            grad_lat_gain[:, None].astype(BF),
+            jnp.zeros((KV, LANES - 1), BF),
+        ],
+        axis=1,
+    )
+    grad_we = lax.psum_scatter(grad_we, "expert", scatter_dimension=0, tiled=True)
+    grad_we = lax.all_gather(grad_we, PLANE, axis=0)
+    grad_lat_gain = jnp.sum(grad_we[:, :, heads * (NOPE + VH)].astype(F32), axis=0)
+    grad_we = columns_of(grad_we[:, :, : heads * (NOPE + VH)]).astype(F32)
     own_cos, own_sin = own_rows(cosine), own_rows(sine_part)
     former, latter = grad_lat[:, KV : KV + ROPE // 2], grad_lat[:, KV + ROPE // 2 : lat_cols]
     own_latent = jnp.concatenate(
@@ -893,60 +1345,39 @@
     grad_tokens, grad_attn = norm_back(grad_h1, normed_one, factor_one, attn_gain)
     grad_inputs = (grad_first + grad_tokens).astype(BF)[None]
 
-    grads = jnp.concatenate(
-        [grad_wq.astype(BF), grad_wo.reshape(width, out_cols).astype(BF), grad_wl.astype(BF)],
+    late_cols = query_cols + lat_cols // 4
+    late = jnp.concatenate(
+        [
+            grad_wq.astype(BF),
+            grad_wl.astype(BF),
+            grad_attn[:, None].astype(BF),
+            jnp.zeros((width, -(late_cols + 1) % LANES), BF),
+        ],
         axis=1,
     )
-    grads = lax.psum_scatter(grads, "expert", scatter_dimension=0, tiled=True)
-    grads = lax.all_gather(grads, PLANE, axis=0)
-    grad_we = lax.psum_scatter(grad_we.astype(BF), "expert", scatter_dimension=0, tiled=True)
-    grad_we = lax.all_gather(grad_we, PLANE, axis=1, tiled=True).astype(F32)
+    late = finish(late.reshape(nz, 2, local_rows, -1), nz, 13).reshape(4, local_rows, -1)
     grad_wq = jnp.concatenate(
         [
-            grads[:, :, :nope_cols].reshape(4, local_rows, heads, NOPE),
-            grads[:, :, nope_cols : nope_cols + rope_cols].reshape(4, local_rows, heads, -1),
-            grads[:, :, nope_cols + rope_cols : query_cols].reshape(4, local_rows, heads, -1),
+            late[:, :, :nope_cols].reshape(4, local_rows, heads, NOPE),
+            late[:, :, nope_cols : nope_cols + rope_cols].reshape(4, local_rows, heads, -1),
+            late[:, :, nope_cols + rope_cols : query_cols].reshape(4, local_rows, heads, -1),
         ],
         axis=3,
     )
     grad_wq = columns_of(grad_wq.reshape(4, local_rows, -1)).astype(F32)
-    grad_wo = columns_of(grads[:, :, query_cols : query_cols + out_cols]).astype(F32)
-    grad_wl = columns_of(grads[:, :, query_cols + out_cols :]).astype(F32)
-    shared_in = jnp.concatenate([grad_cat[:units], grad_cat[LANES : LANES + units]], axis=0)
-    shared_in = lax.all_to_all(
-        shared_in.astype(BF).reshape(2 * units, groups, local_rows),
-        "expert",
-        split_axis=1,
-        concat_axis=0,
-        tiled=True,
-    )
-    shared_in = lax.all_gather(shared_in.reshape(-1, local_rows), PLANE, axis=0)
-    shared_in = shared_in.reshape(4, groups, 2, units, local_rows)
-    shared_in = shared_in.transpose(4, 2, 1, 0, 3).reshape(local_rows, -1).astype(F32)
-    shared_out = lax.all_gather(grad_so[:units].astype(BF), PLANE, axis=0, tiled=True).astype(F32)
-    small = jnp.concatenate(
-        [
-            grad_cat[units : units + experts],
-            grad_attn[None],
-            grad_ffn[None],
-            jnp.pad(grad_lat_gain, (0, width - KV))[None],
-        ],
-        axis=0,
-    )
-    small = lax.psum(small, ALL)
-    rows = plane_part(small, spot, 1, groups)
-    lat_rows = plane_part(small[experts + 2, :KV], spot, 0, groups)
+    grad_wl = columns_of(late[:, :, query_cols:late_cols]).astype(F32)
+    grad_attn = jnp.sum(late[:, :, late_cols].astype(F32), axis=0)
     return (
         output,
         grad_inputs,
-        rows[experts],
+        grad_attn,
         grad_wq,
         grad_wl,
-        lat_rows,
+        grad_lat_gain,
         grad_we,
         grad_wo,
-        rows[experts + 1],
-        rows[:experts].T,
+        grad_ffn,
+        grad_wr,
         shared_in,
         shared_out,
         grad_in,

time: 1130 us -> 928 us (0.82)
  waiting for transfers between devices: 189 us -> 48.5 us
  blocking collectives: 136 us -> 10.1 us
  Pallas kernels: 602 us -> 631 us
  local copies, waits for them, and re-layouts: 89.1 us -> 116 us
    all_gather x2 -> x1, blocking collectives: 102 us -> 10.1 us  [split_body(): grad_we = lax.all_gather(grad_we, PLANE, axis=0)]
    psum x1 -> x0, waiting for transfers between devices: 59.8 us -> none  [split_body(): small = lax.psum(small, ALL)]
    all_gather x1, waiting for transfers between devices: 40.3 us -> 0.01 us  [split_body(): shared_in = lax.all_gather(shared_in.reshape(-1, local_rows), PLANE, axis=0)]
    reduce_scatter x2, waiting for transfers between devices: 37.7 us -> 0.01 us  [the longest x1 0.01 us: split_body(): early = lax.psum_scatter(early, 'expert', scatter_dimension=0, tiled=True)]
    all_to_all x1 -> x0, blocking collectives: 34.6 us -> none  [split_body(): lax.all_to_all(shared_in.astype(BF).reshape(2 * units, groups, local_rows...]
    all_gather x2, waiting for transfers between devices: 31.6 us -> 0.02 us  [the longest x1 0.02 us: split_body(): lax.all_gather(jnp.concatenate([cotangent[0], named_here.astype(BF)], axi...]
    all_gather x1, waiting for transfers between devices: 0.01 us -> 29.3 us  [split_body(): attn_w = lax.all_gather(attn_pack, 'expert', axis=0, tiled=True)]
    pallas_call x1, Pallas kernels: 86.3 us -> 110 us  [gather_all(): pl.pallas_call(functools.partial(gather_all_kernel, nz, rows), out_shape=...]
  transfers between devices with their start and end apart: 10 -> 9, of which waited for: 6 -> 3; matrix products, arithmetic and copies ran while one was open for 9% -> 16% of each run, Pallas kernels for 24% -> 35%
where the time goes in v2:
time: 928 us; the launch traced here: 912 us
  Pallas kernels  631 us (68%)
  local copies, waits for them, and re-layouts  116 us (12%)
  waiting for transfers between devices  48.5 us (5%)
  other arithmetic  47.5 us (5%)
  matrix products  36.6 us (4%)
  between operations  15.4 us (2%)
  blocking collectives  10.1 us (1%)
    pallas_call x1, Pallas kernels, ffn(): pl.pallas_call(functools.partial(ffn_kernel, (nz, tok, hidden, padded, sl...  304 us
    pallas_call x1, Pallas kernels, gather_all(): pl.pallas_call(functools.partial(gather_all_kernel, nz, rows), out_shape=...  110 us
    pallas_call x3, Pallas kernels, gather_plane(): pl.pallas_call(functools.partial(gather_plane_kernel, rows), out_shape=ja...  63.2 us
    pallas_call x1, Pallas kernels, finish(): pl.pallas_call(functools.partial(finish_kernel, nz, rows), out_shape=jax....  62.9 us
    pallas_call x3, Pallas kernels, sum_plane(): pl.pallas_call(functools.partial(sum_plane_kernel, rows), out_shape=jax.S...  48 us
    unnamed x129, local copies, waits for them, and re-layouts  39 us
    all_gather x1, waiting for transfers between devices, split_body(): attn_w = lax.all_gather(attn_pack, 'expert', axis=0, tiled=True)  29.3 us
    pallas_call x2, Pallas kernels, swap_plane(): pl.pallas_call(swap_plane_kernel, out_shape=jax.ShapeDtypeStruct(part.sha...  24.7 us
  transfers between devices with their start and end apart: 9, of which 3 were waited for; matrix products, arithmetic and copies ran while one was open for 16% of the time, Pallas kernels for 35%

profile of v2, /device:TPU:0, one launch (start us, length us, event | category | flops | bytes accessed | tf_op | source)
XLA Modules:
  0.0 912.5 jit_solution(10162773032447651612)
XLA Ops:
  19.5 6.4 all-to-all-start
  27.6 24.4 %gather_plane_1.1 = bf16[2,2,128,2048]{3,2,1,0:T(8,128)(2,1)} custom-call(bf16[128,2048]{1,0:T(8,128)(2,1)} %fusion.11.own), custom_call_target="tpu_custom_call" | custom-call | bytes 66000000 | tf_op jit(solution)/shard_map/gather_plane_1/pallas_call | solution.py:293
  54.0 6.6 pad.12
  62.6 18.2 %all-to-all-done = bf16[8,256,256]{1,2,0:T(8,128)(2,1)} async-done(((bf16[8,256,256]{1,2,0:T(8,128)(2,1)}), bf16[8,256,256]{1,2,0:T(8,128)(2,1)}, u32[]{:S(2)}, u32[]{:S(2)}) %all-to-all-start) | async-done | bytes 1048608 | tf_op jit(solution)/shard_map/all_to_all | solution.py:1204
  83.1 29.3 %all-gather.9.cloned.1.call-done = bf16[2048,1856]{0,1:T(8,128)(2,1)} async-done(((bf16[256,1856]{0,1:T(8,128)(2,1)}), bf16[2048,1856]{0,1:T(8,128)(2,1)}) %all-gather.9.cloned.1.call-update) | async-done | bytes 7602192 | tf_op jit(solution)/shard_map/all_gather | solution.py:1172
  138.5 7.9 attend.1.own
  146.4 28.0 %gather_plane_2.1 = bf16[2,2,512,512]{3,2,1,0:T(8,128)(2,1)} custom-call(bf16[512,512]{1,0:T(8,128)(2,1)} %attend.1.own), custom_call_target="tpu_custom_call" | custom-call | bytes 66000000 | tf_op jit(solution)/shard_map/gather_plane_2/pallas_call | solution.py:293
  177.6 4.1 copy.246
  187.6 15.5 %swap_plane_3.1 = bf16[2,2,128,512]{3,2,1,0:T(8,128)(2,1)} custom-call(bf16[2,2,128,512]{3,2,1,0:T(8,128)(2,1)} %bitcast.199), custom_call_target="tpu_custom_call" | custom-call | bytes 36000000 | tf_op jit(solution)/shard_map/swap_plane_3/pallas_call | solution.py:323
  207.5 109.8 %gather_all_4.1 = bf16[2,2,4,2,128,2048]{5,4,3,2,1,0:T(8,128)(2,1)} custom-call(bf16[128,2048]{1,0:T(8,128)(2,1)} %multiply_convert_fusion.own), custom_call_target="tpu_custom_call" | custom-call | bytes 258000000 | tf_op jit(solution)/shard_map/gather_all_4/pallas_call | solution.py:133
  321.5 303.8 %ffn.1 = (f32[128,2048]{1,0:T(8,128)}, f32[128,2048]{1,0:T(8,128)}, f32[2,2,352,2048]{3,2,1,0:T(8,128)}, f32[2,352,2048]{2,1,0:T(8,128)}, f32[256,2048]{1,0:T(8,...) custom-call(bf16[4096,2048]{1,0:T(8,128)(2,1)} %bitcast.144, ...), custom_call_target="tpu_custom_call" | custom-call | bytes 600000000 | tf_op jit(solution)/shard_map/ffn/pallas_call | solution.py:968
  632.1 9.3 %swap_plane_7.1 = bf16[2,2,128,512]{3,2,1,0:T(8,128)(2,1)} custom-call(bf16[2,2,128,512]{3,2,1,0:T(8,128)(2,1)} %bitcast.180), custom_call_target="tpu_custom_call" | custom-call | bytes 36000000 | tf_op jit(solution)/shard_map/swap_plane_7/pallas_call | solution.py:323
  644.6 4.1 maximum_maximum_fusion.1
  653.6 4.1 copy.253
  657.8 19.3 %sum_plane_8.1 = f32[512,512]{1,0:T(8,128)} custom-call(bf16[2,2,512,512]{3,2,1,0:T(8,128)(2,1)} %bitcast.159), custom_call_target="tpu_custom_call" | custom-call | bytes 60000000 | tf_op jit(solution)/shard_map/sum_plane_8/pallas_call | solution.py:368
  679.2 10.9 %attend_back.1 = (bf16[512,512]{1,0:T(8,128)(2,1)}, f32[512,128]{1,0:T(8,128)}, f32[512,128]{1,0:T(8,128)}, bf16[512,1024]{1,0:T(8,128)(2,1)}, f32[512,128]{1,0:T(8,128)}, /*index=5*/f32[512,128]{1,0:T(8,128)}) custom-call(bf16[512,512]{1,0:T(8,128)(2,1)} %slice.204.qn, bf16[512,128]{1,0:T(8,128)(2,1)} %get-tuple-element.121.qf, ...), custom_call_target="tpu_custom_call" | custom-call | bytes 33000000 | tf_op jit(solution)/shard_map/attend_back/pallas_call | solution.py:1082
  697.9 10.9 %sum_plane_9.1 = f32[128,640]{1,0:T(8,128)} custom-call(bf16[2,2,128,640]{3,2,1,0:T(8,128)(2,1)} %maximum_maximum_fusion.2.part), custom_call_target="tpu_custom_call" | custom-call | bytes 60000000 | tf_op jit(solution)/shard_map/sum_plane_9/pallas_call | solution.py:368
  718.4 10.8 %gather_plane_10.1 = bf16[2,2,128,640]{3,2,1,0:T(8,128)(2,1)} custom-call(bf16[128,640]{1,0:T(8,128)(2,1)} %maximum_maximum_fusion.3.own), custom_call_target="tpu_custom_call" | custom-call | bytes 66000000 | tf_op jit(solution)/shard_map/gather_plane_10/pallas_call | solution.py:293
  733.9 5.2 convolution_convert_fusion.2
  739.1 17.9 %sum_plane_11.1 = f32[128,2048]{1,0:T(8,128)} custom-call(bf16[2,2,128,2048]{3,2,1,0:T(8,128)(2,1)} %bitcast.174), custom_call_target="tpu_custom_call" | custom-call | bytes 60000000 | tf_op jit(solution)/shard_map/sum_plane_11/pallas_call | solution.py:368
  767.8 62.9 %finish_13.1 = bf16[2,2,256,1024]{3,2,1,0:T(8,128)(2,1)} custom-call(bf16[4,2,256,1024]{3,2,1,0:T(8,128)(2,1)} %maximum_maximum_fusion.part), custom_call_target="tpu_custom_call" | custom-call | bytes 210000000 | tf_op jit(solution)/shard_map/finish_13/pallas_call | solution.py:475
  854.5 10.1 %all-gather = bf16[256,1152]{1,0:T(8,128)(2,1)S(1)} all-gather(bf16[64,1152]{1,0:T(8,128)(2,1)} %reduce-scatter.3.cloned.1.call-done), channel_id=2, replica_groups=mesh['dp'=2,'ctx'=2,'expert'=8] {'dp','ctx'}, dimensions={0}, use_global_device_ids=true | all-gather | bytes 737280 | tf_op jit(solution)/shard_map/all_gather | solution.py:1317
  872.2 6.2 copy.276
  892.1 10.7 %copy.303 = f32[2,2,352,2048]{3,2,1,0:T(8,128)} copy(f32[2,2,352,2048]{3,2,1,0:T(8,128)} %get-tuple-element.171) | data formatting | bytes 23068672
  (277 shorter events, 160.8 us)
Async XLA Ops:
  7.2 105.2 %all-gather.9.cloned.1.call-start = ((), (), s32[]{:S(2)}) async-start(), calls=%async_computation.3 | async-start | bytes 8552448 | tf_op jit(solution)/shard_map/all_gather | solution.py:1172
  10.8 124.6 %all-gather.11.cloned.1.call-start = ((), (), s32[]{:S(2)}) async-start(), calls=%async_computation.4 | async-start | bytes 1179648 | tf_op jit(solution)/shard_map/all_gather | solution.py:1173
  11.6 305.7 %all-gather.13.cloned.1.call-start = ((), (), s32[]{:S(2)}) async-start(), calls=%async_computation.5 | async-start | bytes 18382848 | tf_op jit(solution)/shard_map/all_gather | solution.py:1180
  19.5 61.4 %all-to-all-start = ((bf16[8,256,256]{1,2,0:T(8,128)(2,1)}), bf16[8,256,256]{1,2,0:T(8,128)(2,1)}, u32[]{:S(2)}, u32[]{:S(2)}) async-start(bf16[8,256,256]{1,2,0:T(8,128)(2,1)} %bitcast.29), calls=%async_computation | async-start | bytes 2097152 | tf_op jit(solution)/shard_map/all_to_all | solution.py:1204
  25.8 813.3 %reduce-scatter.5.cloned.1.call-start = ((), (), s32[]{:S(2)}) async-start(), calls=%async_computation.7 | async-start | bytes 2949120 | tf_op jit(solution)/shard_map/reduce_scatter | solution.py:1280
  62.5 49.9 %copy-start.5 = (bf16[2,2,128,2048]{3,2,1,0:T(8,128)(2,1)S(1)}, bf16[2,2,128,2048]{3,2,1,0:T(8,128)(2,1)}, u32[]{:S(2)}) copy-start(bf16[2,2,128,2048]{3,2,1,0:T(8,128)(2,1)} %gather_plane_1.1) | copy-start | bytes 6291460
  118.8 14.5 %copy-start.26 = (f32[512,32]{1,0:T(8,128)}, f32[512,32]{1,0:T(8,128)S(1)}, u32[]{:S(2)}) copy-start(f32[512,32]{1,0:T(8,128)S(1)} %get-tuple-element.139) | copy-start | bytes 196612
  122.6 11.6 %copy-start.21 = (f32[512,128]{1,0:T(8,128)}, f32[512,128]{1,0:T(8,128)S(1)}, u32[]{:S(2)}) copy-start(f32[512,128]{1,0:T(8,128)S(1)} %copy.236) | copy-start | bytes 786436
  135.2 11.2 %copy-start.7 = (f32[512,512]{1,0:T(8,128)}, f32[512,512]{1,0:T(8,128)S(1)}, u32[]{:S(2)}) copy-start(f32[512,512]{1,0:T(8,128)S(1)} %slice_multiply_fusion) | copy-start | bytes 3145732
  205.6 421.7 %copy-start.45 = (f32[128]{0:T(128)}, f32[128]{0:T(128)S(1)}, u32[]{:S(2)}) copy-start(f32[128]{0:T(128)S(1)} %add_rsqrt_fusion.1) | copy-start | bytes 1540
  629.6 12.7 %copy-start.23 = (bf16[4,512,512]{1,2,0:T(8,128)(2,1)S(1)}, bf16[4,512,512]{1,2,0:T(8,128)(2,1)}, u32[]{:S(2)}) copy-start(bf16[4,512,512]{1,2,0:T(8,128)(2,1)} %copy.272) | copy-start | bytes 6291460
  648.8 202.3 %all-gather.17.cloned.1.call-start = ((), (), s32[]{:S(2)}) async-start(), calls=%async_computation.9 | async-start | bytes 1802240 | tf_op jit(solution)/shard_map/all_gather | solution.py:1260
  650.9 203.6 %reduce-scatter.3.cloned.1.call-start = ((), (), s32[]{:S(2)}) async-start(), calls=%async_computation.6 | async-start | bytes 1327104 | tf_op jit(solution)/shard_map/reduce_scatter | solution.py:1316
  651.0 45.0 %copy-start.41 = (bf16[640]{0:T(1024)(128)(2,1)}, bf16[640]{0:T(1024)(128)(2,1)S(1)}, u32[]{:S(2)}) copy-start(bf16[640]{0:T(1024)(128)(2,1)S(1)} %pad.36.clone) | copy-start | bytes 3844
  679.2 14.7 %copy-start.27 = (bf16[512,1024]{1,0:T(8,128)(2,1)S(1)}, bf16[512,1024]{1,0:T(8,128)(2,1)}, u32[]{:S(2)}) copy-start(bf16[512,1024]{1,0:T(8,128)(2,1)} %all-gather.11.cloned.1.call-done) | copy-start | bytes 3145732
  693.8 15.0 %copy-start.8 = (f32[512,512]{1,0:T(8,128)S(1)}, f32[512,512]{1,0:T(8,128)}, u32[]{:S(2)}) copy-start(f32[512,512]{1,0:T(8,128)} %copy-done.7) | copy-start | bytes 3145732
  714.0 15.2 %copy-start.6 = (bf16[2,2,128,2048]{3,2,1,0:T(8,128)(2,1)S(1)}, bf16[2,2,128,2048]{3,2,1,0:T(8,128)(2,1)}, u32[]{:S(2)}) copy-start(bf16[2,2,128,2048]{3,2,1,0:T(8,128)(2,1)} %gather_plane_1.1) | copy-start | bytes 6291460
  714.0 152.4 %all-gather.15.cloned.1.call-start = ((), (), s32[]{:S(2)}) async-start(), calls=%async_computation.8 | async-start | bytes 3604480 | tf_op jit(solution)/shard_map/all_gather | solution.py:1257
  714.8 163.7 %all-gather.19.cloned.1.call-start = ((), (), s32[]{:S(2)}) async-start(), calls=%async_computation.10 | async-start | bytes 1638400 | tf_op jit(solution)/shard_map/all_gather | solution.py:1281
  717.6 11.5 %copy-start.29 = (bf16[128,512]{1,0:T(8,128)(2,1)}, bf16[128,512]{1,0:T(8,128)(2,1)S(1)}, u32[]{:S(2)}) copy-start(bf16[128,512]{1,0:T(8,128)(2,1)S(1)} %multiply_convert_fusion.2) | copy-start | bytes 393220
  739.1 17.9 %copy-start.30 = (bf16[128,512]{1,0:T(8,128)(2,1)S(1)}, bf16[128,512]{1,0:T(8,128)(2,1)}, u32[]{:S(2)}) copy-start(bf16[128,512]{1,0:T(8,128)(2,1)} %copy-done.29) | copy-start | bytes 393220
  739.1 17.9 %copy-start.49 = (f32[128]{0:T(128)S(1)}, f32[128]{0:T(128)}, u32[]{:S(2)}) copy-start(f32[128]{0:T(128)} %copy-done.48) | copy-start | bytes 1540
  888.2 14.7 %slice-start.1 = ((s8[5767168]{0:T(1024)(128)(4,1)}), s8[4194304]{0:T(1024)(128)(4,1)S(1)}, s32[]{:S(2)}) async-start(s8[5767168]{0:T(1024)(128)(4,1)} %bitcast.161), calls=%async_computation.12 | async-start | bytes 8388608
  892.1 10.8 %slice-start.2 = ((s8[5767168]{0:T(1024)(128)(4,1)}), s8[1572864]{0:T(1024)(128)(4,1)S(1)}, s32[]{:S(2)}) async-start(s8[5767168]{0:T(1024)(128)(4,1)} %bitcast.161), calls=%async_computation.13 | async-start | bytes 3145728
  (40 other events, 144.4 us)
Sparse Core Ops, SparseCore 0:
  11.0 101.3 all-gather.8
  114.5 20.8 all-gather.10
  138.8 163.1 all-gather.12
  648.9 35.9 reduce-scatter.4
  687.2 31.5 all-gather.16
  721.5 34.1 reduce-scatter.2
  757.5 43.5 all-gather.14
  839.3 33.0 all-gather.18
